TPU v7x, 32 devices: a whole 2x2x4 slice. The times are simulated.
32 devices in a mesh: grp: 2 (over y), page: 16 (over z, x, core).
Axes of the slice: x: 2, y: 2, z: 4, core: 2. Of those that a mesh axis runs over, the one named last changes fastest.
Arguments:
- queries: bfloat16 [32, 4096], P('grp'), parts along dimension 0, may hold values from -64 to 64
- key_cache: bfloat16 [1024, 64, 1024], P(('grp', 'page')), parts along dimension 0, may hold values from -9 to 9
- value_cache: bfloat16 [1024, 64, 1024], P(('grp', 'page')), parts along dimension 0, may hold values from -16 to 16
- new_keys: bfloat16 [32, 1024], P('grp'), parts along dimension 0, may hold values from -16 to 16
- new_values: bfloat16 [32, 1024], P('grp'), parts along dimension 0, may hold values from -6 to 6
- chosen: int32 [16, 256], P('grp', 'page'), parts along dimension 0, may hold values from 0 to 511, as said below
Outputs:
- attended: bfloat16 [32, 4096], P('grp'), parts along dimension 0
There are 2 independent parts, one for each index of `grp`. A program takes and returns all parts, laid end to end along the dimension named above; each array names one. Nothing has to cross between parts.
Inputs may be any that keep to these rules, and one draw needn't show every extreme that they name: `chosen`: each row names 256 different pages; at most 32 of a row's pages lie in the range of 32 pages of one device, and exactly 32 do for some device in every row.
All inputs are finite; a program needn't handle non-finite values.
Results may differ from a plain program's by a relative error of at most 0.004.
Values may be sent and summed in bfloat16 or wider, within the bound.
No kernel may reach another device: no remote copies, remote signals or barrier semaphores. Data moves between devices by JAX's collectives and lax.ppermute only.
A program may use at most 64 MiB of HBM per device.

v0:
```python
import jax
import jax.numpy as jnp
from jax import lax
from jax.sharding import PartitionSpec as P

FLOOR_SCORE = -1e30


def combine(former, latter):
    high_a, sums_a, weighted_a = former
    high_b, sums_b, weighted_b = latter
    highest = jnp.maximum(high_a, high_b)
    factor_a = jnp.exp(high_a - highest)
    factor_b = jnp.exp(high_b - highest)
    return (
        highest,
        sums_a * factor_a + sums_b * factor_b,
        weighted_a * factor_a[..., None] + weighted_b * factor_b[..., None],
    )


def fresh_term(query_rows, key_rows, value_rows, depth_pos, scaling):
    scores = (
        jnp.einsum("nd,ntd->nt", query_rows, key_rows, preferred_element_type=jnp.float32) * scaling
    )
    allowed = jnp.arange(key_rows.shape[1], dtype=jnp.int32)[None, :] <= depth_pos[:, None]
    highest = jnp.max(jnp.where(allowed, scores, FLOOR_SCORE), axis=1)
    weights = jnp.where(allowed, jnp.exp(scores - highest[:, None]), 0.0).astype(jnp.bfloat16)
    totals = jnp.sum(weights.astype(jnp.float32), axis=1)
    weighted = jnp.einsum("nt,ntd->nd", weights, value_rows, preferred_element_type=jnp.float32)
    return (highest, totals, weighted)


def on_device(queries, key_cache, value_cache, new_keys, new_values, chosen):
    page_count, page_tokens, head_span = key_cache.shape
    chosen_all = lax.all_gather(chosen, "page", axis=1, tiled=True)
    kv_heads = chosen_all.shape[0]
    head_width = head_span // kv_heads
    drafts = queries.shape[0]
    groups = queries.shape[1] // head_span
    row_count = drafts * groups
    scaling = head_width ** (-0.5)
    query_heads = (
        queries.reshape(drafts, kv_heads, groups, head_width)
        .transpose(1, 0, 2, 3)
        .reshape(kv_heads, row_count, head_width)
    )
    local_pages = chosen_all - lax.axis_index("page") * page_count
    page_slots = jnp.arange(page_count, dtype=jnp.int32)
    picked = jnp.any(local_pages[:, :, None] == page_slots[None, None, :], axis=1)
    key_flat = key_cache.reshape(page_count * page_tokens, kv_heads, head_width)
    value_flat = value_cache.reshape(page_count * page_tokens, kv_heads, head_width)
    usable = jnp.repeat(picked, page_tokens, axis=1)
    scores = (
        jnp.einsum("hrd,nhd->hrn", query_heads, key_flat, preferred_element_type=jnp.float32)
        * scaling
    )
    scores = jnp.where(usable[:, None, :], scores, FLOOR_SCORE)
    highest = jnp.max(scores, axis=2)
    present = highest > 0.5 * FLOOR_SCORE
    offset = jnp.where(present, highest, 0.0)
    weights = jnp.where(usable[:, None, :], jnp.exp(scores - offset[..., None]), 0.0).astype(
        jnp.bfloat16
    )
    totals = jnp.sum(weights.astype(jnp.float32), axis=2)
    weighted = jnp.einsum("hrn,nhd->hrd", weights, value_flat, preferred_element_type=jnp.float32)
    all_rows = kv_heads * row_count
    highest = highest.reshape(all_rows)
    totals = totals.reshape(all_rows)
    weighted = weighted.reshape(all_rows, head_width)
    key_heads = new_keys.reshape(drafts, kv_heads, head_width).transpose(1, 0, 2)
    value_heads = new_values.reshape(drafts, kv_heads, head_width).transpose(1, 0, 2)
    query_flat = query_heads.reshape(all_rows, head_width)
    devices = lax.axis_size("page")
    share_rows = all_rows // devices
    pieces = (
        highest.reshape(devices, share_rows),
        totals.reshape(devices, share_rows),
        weighted.reshape(devices, share_rows, head_width),
    )
    high_in, sums_in, weighted_in = (
        lax.all_to_all(pieces[0], "page", split_axis=0, concat_axis=0, tiled=True),
        lax.all_to_all(pieces[1], "page", split_axis=0, concat_axis=0, tiled=True),
        lax.all_to_all(pieces[2], "page", split_axis=0, concat_axis=0, tiled=True),
    )
    merged_high = jnp.max(high_in, axis=0)
    factors = jnp.exp(high_in - merged_high[None, :])
    merged = (
        merged_high,
        jnp.sum(sums_in * factors, axis=0),
        jnp.sum(weighted_in * factors[..., None], axis=0),
    )
    first_row = lax.axis_index("page") * share_rows
    row_ids = first_row + jnp.arange(share_rows, dtype=jnp.int32)
    query_own = lax.dynamic_slice_in_dim(query_flat, first_row, share_rows, 0)
    head_ids = row_ids // row_count
    depth_pos = row_ids % row_count // groups
    fresh = fresh_term(query_own, key_heads[head_ids], value_heads[head_ids], depth_pos, scaling)
    final_high, final_sums, final_weighted = combine(merged, fresh)
    finished = (final_weighted / final_sums[:, None]).astype(jnp.bfloat16)
    result = lax.all_gather(finished, "page", axis=0, tiled=True)
    return (
        result.reshape(kv_heads, drafts, groups, head_width)
        .transpose(1, 0, 2, 3)
        .reshape(drafts, kv_heads * groups * head_width)
    )


def solution(mesh):
    placed = (
        P("grp", None),
        P(("grp", "page"), None, None),
        P(("grp", "page"), None, None),
        P("grp", None),
        P("grp", None),
        P("grp", "page"),
    )
    return jax.shard_map(
        on_device, mesh=mesh, in_specs=placed, out_specs=P("grp", None), check_vma=False
    )
```

profile of v0, /device:TPU:0, one launch (start us, length us, event | category | flops | bytes accessed | tf_op | source)
XLA Modules:
  0.0 91.0 jit_solution(6589487834992607965)
XLA Ops:
  0.0 1.0 %reshape.167 = bf16[16,8,4,128]{3,2,1,0:T(4,128)(2,1)S(1)} reshape(bf16[16,4096]{1,0:T(8,128)(2,1)} %param.6) | data formatting | bytes 262144 | tf_op jit(solution)/shard_map/reshape | solution.py:44
  1.0 23.5 %all-gather = s32[16,16,8]{1,2,0:T(8,128)S(1)} all-gather(s32[1,16,8]{1,2,0:T(8,128)} %bitcast.70), channel_id=1, replica_groups=mesh['grp'=2,'page'=16] {'page'}, dimensions={0}, use_global_device_ids=true | all-gather | bytes 8704 | tf_op jit(solution)/shard_map/all_gather | solution.py:36
  24.7 0.2 fusion.5
  25.0 0.1 broadcast_in_dim.48
  25.1 3.3 %copy.42 = bf16[256,8,8,128]{3,2,1,0:T(8,128)(2,1)S(1)} copy(bf16[256,8,8,128]{3,1,2,0:T(8,128)(2,1)} %bitcast.60) | data formatting | bytes 8388608
  28.4 1.7 %fusion.4 = (f32[8,64]{1,0:T(8,128)S(1)}, f32[8,64,2048]{2,1,0:T(8,128)S(1)}) fusion(pred[8,2048]{1,0:T(8,128)(4,1)S(1)} %broadcast_in_dim.48, bf16[8,64,128]{2,1,0:T(8,128)(2,1)S(1)} %bitcast.63, bf16[2048,8,128]{2,1,0:T(8,128)(2,1)S(1)} %bitcast.59), kind=kOutput, calls=%fused_computation.9 | convolution fusion | flops 271580672 | bytes 8538112 | tf_op jit(solution)/shard_map/hrd,nhd->hrn/dot_general | solution.py:55
  30.2 1.9 %copy-done.1 = f32[8,64,2048]{2,1,0:T(8,128)} copy-done((f32[8,64,2048]{2,1,0:T(8,128)}, f32[8,64,2048]{2,1,0:T(8,128)S(1)}, u32[]{:S(2)}) %copy-start.1) | copy-done | bytes 4194328
  32.1 1.3 %convert_reduce_fusion = f32[8,64]{1,0:T(8,128)S(1)} fusion(f32[8,64]{1,0:T(8,128)S(1)} %compare_select_fusion, f32[8,64,2048]{2,1,0:T(8,128)S(1)} %get-tuple-element.13, pred[8,2048]{1,0:T(8,128)(4,1)S(1)} %broadcast_in_dim.48), kind=kLoop, calls=%fused_computation.6 | loop fusion | flops 7339520 | bytes 4214784 | tf_op jit(solution)/shard_map/reduce_sum | solution.py:65
  33.4 0.7 all_to_all.23
  34.1 3.5 %all-to-all-start.2 = ((f32[16,1,32]{2,1,0:T(1,128)}), f32[16,1,32]{2,1,0:T(1,128)S(1)}, u32[]{:S(2)}, u32[]{:S(2)}) async-start(f32[16,1,32]{2,1,0:T(1,128)} %all_to_all.23), calls=%async_computation.2 | async-start | bytes 16384 | tf_op jit(solution)/shard_map/all_to_all | solution.py:83
  37.7 0.6 gather_fusion
  38.2 0.2 fusion.6
  38.5 3.5 %copy.43 = bf16[256,8,8,128]{3,2,1,0:T(8,128)(2,1)S(1)} copy(bf16[256,8,8,128]{3,1,2,0:T(8,128)(2,1)} %bitcast.61) | data formatting | bytes 8388608
  42.0 2.5 %fusion = f32[8,64,128]{2,1,0:T(8,128)} fusion(bf16[2048,8,128]{2,1,0:T(8,128)(2,1)S(1)} %bitcast.62, f32[8,64,2048]{2,1,0:T(8,128)S(1)} %copy-done.2, f32[8,64]{1,0:T(8,128)S(1)} %compare_select_fusion, pred[8,2048]{1,0:T(8,128)(4,1)S(1)} %broadcast_in_dim.48), kind=kOutput, calls=%fused_computation.2 | convolution fusion | flops 273678336 | bytes 8669184 | tf_op jit(solution)/shard_map/hrn,nhd->hrd/dot_general | solution.py:66
  44.5 0.7 all_to_all.20
  45.2 6.0 %all-to-all-start.1 = ((f32[16,1,32]{2,1,0:T(1,128)}), f32[16,1,32]{2,1,0:T(1,128)S(1)}, u32[]{:S(2)}, u32[]{:S(2)}) async-start(f32[16,1,32]{2,1,0:T(1,128)} %all_to_all.20), calls=%async_computation.1 | async-start | bytes 16384 | tf_op jit(solution)/shard_map/all_to_all | solution.py:82
  51.3 0.6 gather_fusion.1
  51.9 5.7 %all-to-all-done.1 = f32[16,1,32]{2,1,0:T(1,128)S(1)} async-done(((f32[16,1,32]{2,1,0:T(1,128)}), f32[16,1,32]{2,1,0:T(1,128)S(1)}, u32[]{:S(2)}, u32[]{:S(2)}) %all-to-all-start.1) | async-done | bytes 2080 | tf_op jit(solution)/shard_map/all_to_all | solution.py:82
  57.6 3.5 %all-to-all-start = ((f32[16,32,128]{2,1,0:T(8,128)}), f32[16,32,128]{2,1,0:T(8,128)S(1)}, u32[]{:S(2)}, u32[]{:S(2)}) async-start(f32[16,32,128]{2,1,0:T(8,128)} %bitcast.5), calls=%async_computation | async-start | bytes 524288 | tf_op jit(solution)/shard_map/all_to_all | solution.py:84
  61.1 0.2 fusion.15
  61.4 9.7 %all-to-all-done = f32[16,32,128]{2,1,0:T(8,128)S(1)} async-done(((f32[16,32,128]{2,1,0:T(8,128)}), f32[16,32,128]{2,1,0:T(8,128)S(1)}, u32[]{:S(2)}, u32[]{:S(2)}) %all-to-all-start) | async-done | bytes 262176 | tf_op jit(solution)/shard_map/all_to_all | solution.py:84
  71.1 0.1 multiply_reduce_fusion
  71.3 18.9 %all_gather.7 = bf16[512,128]{1,0:T(8,128)(2,1)S(1)} all-gather(bf16[32,128]{1,0:T(8,128)(2,1)S(1)} %divide_convert_fusion), channel_id=1, replica_groups=mesh['grp'=2,'page'=16] {'page'}, dimensions={0}, use_global_device_ids=true | all-gather | bytes 139264 | tf_op jit(solution)/shard_map/all_gather | solution.py:101
  90.3 0.7 reshape.174
  (29 shorter events, 0.8 us)
Async XLA Ops:
  0.0 37.6 %copy-start = (bf16[16,1024]{1,0:T(8,128)(2,1)S(1)}, bf16[16,1024]{1,0:T(8,128)(2,1)}, u32[]{:S(2)}) copy-start(bf16[16,1024]{1,0:T(8,128)(2,1)} %param.9) | copy-start | bytes 98308
  30.2 1.9 %copy-start.1 = (f32[8,64,2048]{2,1,0:T(8,128)}, f32[8,64,2048]{2,1,0:T(8,128)S(1)}, u32[]{:S(2)}) copy-start(f32[8,64,2048]{2,1,0:T(8,128)S(1)} %get-tuple-element.13) | copy-start | bytes 12582916
  34.1 11.1 %all-to-all-start.2 = ((f32[16,1,32]{2,1,0:T(1,128)}), f32[16,1,32]{2,1,0:T(1,128)S(1)}, u32[]{:S(2)}, u32[]{:S(2)}) async-start(f32[16,1,32]{2,1,0:T(1,128)} %all_to_all.23), calls=%async_computation.2 | async-start | bytes 16384 | tf_op jit(solution)/shard_map/all_to_all | solution.py:83
  38.5 3.5 %copy-start.2 = (f32[8,64,2048]{2,1,0:T(8,128)S(1)}, f32[8,64,2048]{2,1,0:T(8,128)}, u32[]{:S(2)}) copy-start(f32[8,64,2048]{2,1,0:T(8,128)} %copy-done.1) | copy-start | bytes 12582916
  42.0 2.5 %copy-start.3 = (bf16[16,1024]{1,0:T(8,128)(2,1)S(1)}, bf16[16,1024]{1,0:T(8,128)(2,1)}, u32[]{:S(2)}) copy-start(bf16[16,1024]{1,0:T(8,128)(2,1)} %param.10) | copy-start | bytes 98308
  45.2 12.4 %all-to-all-start.1 = ((f32[16,1,32]{2,1,0:T(1,128)}), f32[16,1,32]{2,1,0:T(1,128)S(1)}, u32[]{:S(2)}, u32[]{:S(2)}) async-start(f32[16,1,32]{2,1,0:T(1,128)} %all_to_all.20), calls=%async_computation.1 | async-start | bytes 16384 | tf_op jit(solution)/shard_map/all_to_all | solution.py:82
  57.6 13.5 %all-to-all-start = ((f32[16,32,128]{2,1,0:T(8,128)}), f32[16,32,128]{2,1,0:T(8,128)S(1)}, u32[]{:S(2)}, u32[]{:S(2)}) async-start(f32[16,32,128]{2,1,0:T(8,128)} %bitcast.5), calls=%async_computation | async-start | bytes 524288 | tf_op jit(solution)/shard_map/all_to_all | solution.py:84
where the time goes:
time: 91.4 us; the launch traced here: 91 us
  blocking collectives  42.5 us (46%)
  waiting for transfers between devices  15.5 us (17%)
  local copies, waits for them, and re-layouts  13.5 us (15%)
  starting transfers between devices  13 us (14%)
  matrix products  4.53 us (5%)
  other arithmetic  1.9 us (2%)
    all_gather x1, blocking collectives, on_device(): chosen_all = lax.all_gather(chosen, 'page', axis=1, tiled=True)  23.5 us
    all_gather x1, blocking collectives, on_device(): result = lax.all_gather(finished, 'page', axis=0, tiled=True)  18.9 us
    all_to_all x1, waiting for transfers between devices, on_device(): lax.all_to_all(pieces[2], 'page', split_axis=0, concat_axis=0, tiled=True)  9.74 us
    unnamed x10, local copies, waits for them, and re-layouts  8.68 us
    all_to_all x1, starting transfers between devices, on_device(): lax.all_to_all(pieces[0], 'page', split_axis=0, concat_axis=0, tiled=True)  5.97 us
    all_to_all x1, waiting for transfers between devices, on_device(): lax.all_to_all(pieces[0], 'page', split_axis=0, concat_axis=0, tiled=True)  5.72 us
    all_to_all x1, starting transfers between devices, on_device(): lax.all_to_all(pieces[2], 'page', split_axis=0, concat_axis=0, tiled=True)  3.53 us
    all_to_all x1, starting transfers between devices, on_device(): lax.all_to_all(pieces[1], 'page', split_axis=0, concat_axis=0, tiled=True)  3.47 us
  transfers between devices with their start and end apart: 3, of which 2 were waited for; matrix products, arithmetic and copies ran while one was open for 9% of the time, Pallas kernels for 0%

commit v1 on v0

v1 whole, which is shorter than its diff:
```python
import jax
import jax.numpy as jnp
from jax import lax
from jax.experimental import pallas as pl
from jax.experimental.pallas import tpu as pltpu
from jax.sharding import PartitionSpec as P

ABSENT = -1e30
LOG2E = 1.4426950408889634
LANES = 128
STATS = 8


def vmem():
    return pl.BlockSpec(memory_space=pltpu.VMEM)


def spread_kernel(page_count, chosen_ref, wanted_ref):
    devices = wanted_ref.shape[0]
    kv_heads, listed = chosen_ref.shape
    chosen = chosen_ref[...]
    lane = lax.broadcasted_iota(jnp.int32, (kv_heads, LANES), 1)
    columns = [jnp.broadcast_to(chosen[:, j : j + 1], (kv_heads, LANES)) for j in range(listed)]

    def one_device(device, carry):
        page = jnp.where(lane < page_count, lane + device * page_count, -1)
        hit = columns[0] == page
        for column in columns[1:]:
            hit = jnp.logical_or(hit, column == page)
        own = jnp.logical_and(lane == page_count, device == 0)
        wanted_ref[device] = jnp.where(jnp.logical_or(hit, own), 1.0, 0.0)
        return carry

    lax.fori_loop(0, devices, one_device, 0)


def head_queries(queries_ref, head, groups):
    width = LANES
    return jnp.concatenate(
        [
            queries_ref[:, (head * groups + g) * width : (head * groups + g + 1) * width]
            for g in range(groups)
        ],
        axis=0,
    )


def padded_rows(rows):
    return jnp.concatenate(
        [rows, jnp.zeros((LANES - rows.shape[0], rows.shape[1]), rows.dtype)], axis=0
    )


def attend_kernel(
    wanted_ref, queries_ref, keys_ref, values_ref, new_keys_ref, new_values_ref, out_ref
):
    page_count, page_tokens, head_span = keys_ref.shape
    tokens = page_count * page_tokens
    kv_heads = wanted_ref.shape[1]
    drafts = queries_ref.shape[0]
    groups = queries_ref.shape[1] // head_span
    rows = drafts * groups
    devices, piece, width = out_ref.shape
    share = piece - STATS
    pieces = rows // share
    scale = width ** (-0.5) * LOG2E
    wanted = jnp.sum(wanted_ref[...], axis=0)
    bias = jnp.where(wanted > 0.5, 0.0, ABSENT)
    slot = lax.broadcasted_iota(jnp.int32, (LANES, tokens), 0)
    token_page = lax.broadcasted_iota(jnp.int32, (LANES, tokens), 1) // page_tokens
    expand = jnp.where(slot == token_page, 1.0, 0.0).astype(jnp.bfloat16)
    flags = jnp.where(wanted > 0.5, 1.0, 0.0).astype(jnp.bfloat16)
    token_flags = jnp.dot(flags, expand, preferred_element_type=jnp.float32)
    token_bias = jnp.where(token_flags > 0.5, 0.0, ABSENT)
    position = lax.broadcasted_iota(jnp.int32, (rows, LANES), 0) % drafts
    lane = lax.broadcasted_iota(jnp.int32, (rows, LANES), 1)
    causal = jnp.where(lane <= position, 0.0, ABSENT)
    stats = jnp.zeros((rows, LANES), jnp.float32)
    contract = (((1,), (1,)), ((), ()))
    for h in range(kv_heads):
        span = slice(h * width, (h + 1) * width)
        query_rows = head_queries(queries_ref, h, groups)
        keys = keys_ref[:, :, span].reshape(tokens, width)
        scores = lax.dot_general(query_rows, keys, contract, preferred_element_type=jnp.float32)
        scores = scores * scale + token_bias[h : h + 1, :]
        fresh = lax.dot_general(
            query_rows, padded_rows(new_keys_ref[:, span]), contract,
            preferred_element_type=jnp.float32,
        )
        fresh = fresh * scale + causal + bias[h : h + 1, page_count : page_count + 1]
        highest = jnp.maximum(
            jnp.max(scores, axis=1, keepdims=True), jnp.max(fresh, axis=1, keepdims=True)
        )
        present = highest > 0.5 * ABSENT
        offset = jnp.where(present, highest, 0.0).astype(jnp.bfloat16).astype(jnp.float32)
        weights = jnp.exp2(scores - offset).astype(jnp.bfloat16)
        fresh_weights = jnp.exp2(fresh - offset).astype(jnp.bfloat16)
        totals = jnp.sum(weights.astype(jnp.float32), axis=1, keepdims=True) + jnp.sum(
            fresh_weights.astype(jnp.float32), axis=1, keepdims=True
        )
        values = values_ref[:, :, span].reshape(tokens, width)
        weighted = jnp.dot(weights, values, preferred_element_type=jnp.float32)
        weighted = weighted + jnp.dot(
            fresh_weights, padded_rows(new_values_ref[:, span]), preferred_element_type=jnp.float32
        )
        weighted = weighted.astype(jnp.bfloat16)
        for i in range(pieces):
            out_ref[h * pieces + i, :share, :] = weighted[i * share : (i + 1) * share]
        coarse = totals.astype(jnp.bfloat16).astype(jnp.float32)
        level = jnp.where(present, offset, ABSENT)
        stats = jnp.where(lane == h * STATS, level, stats)
        stats = jnp.where(lane == h * STATS + 1, coarse, stats)
        stats = jnp.where(lane == h * STATS + 2, totals - coarse, stats)
    turned = padded_rows(stats).T
    for i in range(pieces):
        part = turned if i == 0 else pltpu.roll(turned, LANES - i * share, 1)
        part = part.astype(jnp.bfloat16)
        for h in range(kv_heads):
            out_ref[h * pieces + i, share:, :] = part[h * STATS : (h + 1) * STATS]


def merge_kernel(pieces_ref, out_ref):
    devices, piece, width = pieces_ref.shape
    share = piece - STATS
    stats = jnp.concatenate(
        [pieces_ref[d, share:, :].astype(jnp.float32) for d in range(devices)], axis=0
    )
    if devices * STATS < LANES:
        stats = jnp.concatenate(
            [stats, jnp.zeros((LANES - devices * STATS, width), jnp.float32)], axis=0
        )
    turned = stats.T[:share]
    levels = [turned[:, d * STATS : d * STATS + 1] for d in range(devices)]
    highest = levels[0]
    for level in levels[1:]:
        highest = jnp.maximum(highest, level)
    totals = jnp.zeros((share, 1), jnp.float32)
    weighted = jnp.zeros((share, width), jnp.float32)
    for d in range(devices):
        factor = jnp.exp2(levels[d] - highest)
        sums = (
            turned[:, d * STATS + 1 : d * STATS + 2] + turned[:, d * STATS + 2 : d * STATS + 3]
        )
        totals = totals + sums * factor
        weighted = weighted + pieces_ref[d, :share, :].astype(jnp.float32) * factor
    finished = (weighted / totals).astype(jnp.bfloat16)
    for d in range(devices):
        out_ref[d] = finished


def exchange(pieces):
    return lax.all_to_all(pieces, "page", split_axis=0, concat_axis=0, tiled=True)


def on_device(queries, key_cache, value_cache, new_keys, new_values, chosen):
    page_count, _, head_span = key_cache.shape
    kv_heads = chosen.shape[0]
    width = head_span // kv_heads
    drafts = queries.shape[0]
    groups = queries.shape[1] // head_span
    rows = drafts * groups
    devices = lax.axis_size("page")
    share = kv_heads * rows // devices
    f32 = jnp.float32
    bf16 = jnp.bfloat16
    limit = pltpu.CompilerParams(vmem_limit_bytes=24 * 1024 * 1024)

    wanted = pl.pallas_call(
        lambda *refs: spread_kernel(page_count, *refs),
        out_shape=jax.ShapeDtypeStruct((devices, kv_heads, LANES), f32),
        in_specs=[vmem()],
        out_specs=vmem(),
        compiler_params=limit,
        name="spread",
    )(chosen)
    wanted = exchange(wanted)
    pieces = pl.pallas_call(
        attend_kernel,
        out_shape=jax.ShapeDtypeStruct((devices, share + STATS, width), bf16),
        in_specs=[vmem()] * 6,
        out_specs=vmem(),
        compiler_params=limit,
        name="attend",
    )(wanted, queries, key_cache, value_cache, new_keys, new_values)
    pieces = exchange(pieces)
    finished = pl.pallas_call(
        merge_kernel,
        out_shape=jax.ShapeDtypeStruct((devices, share, width), bf16),
        in_specs=[vmem()],
        out_specs=vmem(),
        compiler_params=limit,
        name="merge",
    )(pieces)
    result = exchange(finished)
    return (
        result.reshape(kv_heads * groups, drafts, width)
        .transpose(1, 0, 2)
        .reshape(drafts, kv_heads * groups * width)
    )


def solution(mesh):
    placed = (
        P("grp", None),
        P(("grp", "page"), None, None),
        P(("grp", "page"), None, None),
        P("grp", None),
        P("grp", None),
        P("grp", "page"),
    )
    return jax.shard_map(
        on_device, mesh=mesh, in_specs=placed, out_specs=P("grp", None), check_vma=False
    )
```

time: 91.4 us -> 49.3 us (0.54)
  waiting for transfers between devices: 15.5 us -> 0 us
  starting transfers between devices: 13 us -> 0 us
  blocking collectives: 42.5 us -> 35.6 us
  local copies, waits for them, and re-layouts: 13.5 us -> 8.14 us
  Pallas kernels: 0 us -> 5.1 us
  matrix products: 4.53 us -> 0 us
  other arithmetic: 1.9 us -> 0 us
    all_gather x2 -> x0, blocking collectives: 42.5 us -> none  [the longest x1 23.5 us: on_device(): chosen_all = lax.all_gather(chosen, 'page', axis=1, tiled=True)]
    all_to_all x0 -> x3, blocking collectives: none -> 35.6 us  [exchange(): lax.all_to_all(pieces, 'page', split_axis=0, concat_axis=0, tiled=True)]
    all_to_all x3 -> x0, waiting for transfers between devices: 15.5 us -> none  [the longest x1 9.74 us: on_device(): lax.all_to_all(pieces[2], 'page', split_axis=0, concat_axis=0, tiled=True)]
    all_to_all x3 -> x0, starting transfers between devices: 13 us -> none  [the longest x1 5.97 us: on_device(): lax.all_to_all(pieces[0], 'page', split_axis=0, concat_axis=0, tiled=True)]
    pallas_call x0 -> x3, Pallas kernels: none -> 5.1 us  [the longest x1 4.18 us: on_device(): pl.pallas_call(attend_kernel, out_shape=jax.ShapeDtypeStruct((devices, sh...]
    dot_general x4 -> x0, matrix products: 4.53 us -> none  [the longest x1 2.46 us: on_device(): jnp.einsum('hrn,nhd->hrd', weights, value_flat, preferred_element_type=jn...]
    reduce_sum x4 -> x0, other arithmetic: 1.48 us -> none  [the longest x1 1.3 us: on_device(): totals = jnp.sum(weights.astype(jnp.float32), axis=2)]
    all_to_all x2 -> x0, local copies, waits for them, and re-layouts: 1.35 us -> none  [the longest x1 0.68 us: on_device(): lax.all_to_all(pieces[1], 'page', split_axis=0, concat_axis=0, tiled=True)]
  transfers between devices with their start and end apart: 3 -> 0, of which waited for: 2 -> 0; matrix products, arithmetic and copies ran while one was open for 9% -> 0% of each run, Pallas kernels for 0% -> 0%
where the time goes in v1:
time: 49.3 us; the launch traced here: 48.9 us
  blocking collectives  35.6 us (72%)
  local copies, waits for them, and re-layouts  8.14 us (17%)
  Pallas kernels  5.1 us (10%)
    all_to_all x3, blocking collectives, exchange(): lax.all_to_all(pieces, 'page', split_axis=0, concat_axis=0, tiled=True)  35.6 us
    unnamed x12, local copies, waits for them, and re-layouts  7.48 us
    pallas_call x1, Pallas kernels, on_device(): pl.pallas_call(attend_kernel, out_shape=jax.ShapeDtypeStruct((devices, sh...  4.18 us

profile of v1, /device:TPU:0, one launch (start us, length us, event | category | flops | bytes accessed | tf_op | source)
XLA Modules:
  0.0 48.9 jit_solution(14703749773586105258)
XLA Ops:
  0.0 0.0 copy-start.5
  0.0 0.7 %copy-done.5 = s32[8,16]{1,0:T(8,128)S(1)} copy-done((s32[8,16]{1,0:T(8,128)S(1)}, s32[8,16]{1,0:T(8,128)}, u32[]{:S(2)}) %copy-start.5) | copy-done | bytes 536
  0.7 0.3 spread.1
  1.0 14.1 %all_to_all.15.wanted_ref = f32[16,8,128]{2,1,0:T(8,128)S(1)} all-to-all(f32[16,8,128]{2,1,0:T(8,128)S(1)} %spread.1), channel_id=1, replica_groups=mesh['grp'=2,'page'=16] {'page'}, dimensions={0} | all-to-all | bytes 131072 | tf_op jit(solution)/shard_map/all_to_all | solution.py:152
  15.1 0.0 copy-start
  15.1 2.2 %copy-done = bf16[32,64,1024]{2,1,0:T(8,128)(2,1)S(1)} copy-done((bf16[32,64,1024]{2,1,0:T(8,128)(2,1)S(1)}, bf16[32,64,1024]{2,1,0:T(8,128)(2,1)}, u32[]{:S(2)}) %copy-start) | copy-done | bytes 4194328
  17.3 0.0 copy-start.1
  17.3 2.2 %copy-done.1 = bf16[32,64,1024]{2,1,0:T(8,128)(2,1)S(1)} copy-done((bf16[32,64,1024]{2,1,0:T(8,128)(2,1)S(1)}, bf16[32,64,1024]{2,1,0:T(8,128)(2,1)}, u32[]{:S(2)}) %copy-start.1) | copy-done | bytes 4194328
  19.5 0.0 copy-start.2
  19.5 0.9 %copy-done.2 = bf16[16,4096]{1,0:T(8,128)(2,1)S(1)} copy-done((bf16[16,4096]{1,0:T(8,128)(2,1)S(1)}, bf16[16,4096]{1,0:T(8,128)(2,1)}, u32[]{:S(2)}) %copy-start.2) | copy-done | bytes 131096
  20.4 0.0 copy-start.3
  20.4 0.8 %copy-done.3 = bf16[16,1024]{1,0:T(8,128)(2,1)S(1)} copy-done((bf16[16,1024]{1,0:T(8,128)(2,1)S(1)}, bf16[16,1024]{1,0:T(8,128)(2,1)}, u32[]{:S(2)}) %copy-start.3) | copy-done | bytes 32792
  21.1 0.0 copy-start.4
  21.1 0.8 %copy-done.4 = bf16[16,1024]{1,0:T(8,128)(2,1)S(1)} copy-done((bf16[16,1024]{1,0:T(8,128)(2,1)S(1)}, bf16[16,1024]{1,0:T(8,128)(2,1)}, u32[]{:S(2)}) %copy-start.4) | copy-done | bytes 32792
  21.9 4.2 %attend.1 = bf16[16,40,128]{2,1,0:T(8,128)(2,1)S(1)} custom-call(f32[16,8,128]{2,1,0:T(8,128)S(1)} %all_to_all.15.wanted_ref, bf16[16,4096]{1,0:T(8,128)(2,1)S(1)} %copy-done.2, bf16[32,64,1024]{2,1,0:T(8,128)(2,1)S(1)} %copy-done, bf16[32,64,1024]{2,1,0:T(8,128)(2,1)S(1)} %copy-done.1, bf16[16,1024]{1,0:T(8,128)(2,1)S(1)} %copy-done.3, ...), custom_call_target="tpu_custom_call" | custom-call | tf_op jit(solution)/shard_map/attend/pallas_call | solution.py:177
  26.1 11.0 %all_to_all.16.pieces_ref = bf16[16,40,128]{2,1,0:T(8,128)(2,1)S(1)} all-to-all(bf16[16,40,128]{2,1,0:T(8,128)(2,1)S(1)} %attend.1), channel_id=1, replica_groups=mesh['grp'=2,'page'=16] {'page'}, dimensions={0} | all-to-all | bytes 327680 | tf_op jit(solution)/shard_map/all_to_all | solution.py:152
  37.1 0.6 %merge.1 = bf16[16,32,128]{2,1,0:T(8,128)(2,1)S(1)} custom-call(bf16[16,40,128]{2,1,0:T(8,128)(2,1)S(1)} %all_to_all.16.pieces_ref), custom_call_target="tpu_custom_call" | custom-call | tf_op jit(solution)/shard_map/merge/pallas_call | solution.py:186
  37.7 10.5 %all_to_all.17 = bf16[16,32,128]{2,1,0:T(8,128)(2,1)S(1)} all-to-all(bf16[16,32,128]{2,1,0:T(8,128)(2,1)S(1)} %merge.1), channel_id=1, replica_groups=mesh['grp'=2,'page'=16] {'page'}, dimensions={0} | all-to-all | bytes 262144 | tf_op jit(solution)/shard_map/all_to_all | solution.py:152
  48.2 0.7 %copy.10 = bf16[32,2,8,128]{3,2,0,1:T(8,128)(2,1)} copy(bf16[32,2,8,128]{3,2,1,0:T(8,128)(2,1)S(1)} %bitcast.7) | data formatting | bytes 262144 | tf_op jit(solution)/shard_map/reshape | solution.py:198
Async XLA Ops:
  0.0 0.7 %copy-start.5 = (s32[8,16]{1,0:T(8,128)S(1)}, s32[8,16]{1,0:T(8,128)}, u32[]{:S(2)}) copy-start(s32[8,16]{1,0:T(8,128)} %refs_0_.1) | copy-start | bytes 1540
  15.1 2.2 %copy-start = (bf16[32,64,1024]{2,1,0:T(8,128)(2,1)S(1)}, bf16[32,64,1024]{2,1,0:T(8,128)(2,1)}, u32[]{:S(2)}) copy-start(bf16[32,64,1024]{2,1,0:T(8,128)(2,1)} %keys_ref.1) | copy-start | bytes 12582916
  17.3 2.2 %copy-start.1 = (bf16[32,64,1024]{2,1,0:T(8,128)(2,1)S(1)}, bf16[32,64,1024]{2,1,0:T(8,128)(2,1)}, u32[]{:S(2)}) copy-start(bf16[32,64,1024]{2,1,0:T(8,128)(2,1)} %values_ref.1) | copy-start | bytes 12582916
  19.5 0.9 %copy-start.2 = (bf16[16,4096]{1,0:T(8,128)(2,1)S(1)}, bf16[16,4096]{1,0:T(8,128)(2,1)}, u32[]{:S(2)}) copy-start(bf16[16,4096]{1,0:T(8,128)(2,1)} %queries_ref.1) | copy-start | bytes 393220
  20.4 0.8 %copy-start.3 = (bf16[16,1024]{1,0:T(8,128)(2,1)S(1)}, bf16[16,1024]{1,0:T(8,128)(2,1)}, u32[]{:S(2)}) copy-start(bf16[16,1024]{1,0:T(8,128)(2,1)} %new_keys_ref.1) | copy-start | bytes 98308
  21.1 0.8 %copy-start.4 = (bf16[16,1024]{1,0:T(8,128)(2,1)S(1)}, bf16[16,1024]{1,0:T(8,128)(2,1)}, u32[]{:S(2)}) copy-start(bf16[16,1024]{1,0:T(8,128)(2,1)} %new_values_ref.1) | copy-start | bytes 98308

commit v2 on v1

--- a/solution.py
+++ b/solution.py
@@ -9,10 +9,20 @@
 LOG2E = 1.4426950408889634
 LANES = 128
 STATS = 8
+TILE = 8
+RESIDENT_BYTES = 3 * 2**20
 
 
 def vmem():
     return pl.BlockSpec(memory_space=pltpu.VMEM)
+
+
+def hbm():
+    return pl.BlockSpec(memory_space=pltpu.HBM)
+
+
+def keep_in(space, *arrays):
+    return [pltpu.with_memory_space_constraint(array, space) for array in arrays]
 
 
 def spread_kernel(page_count, chosen_ref, wanted_ref):
@@ -34,36 +44,105 @@
     lax.fori_loop(0, devices, one_device, 0)
 
 
-def head_queries(queries_ref, head, groups):
-    width = LANES
-    return jnp.concatenate(
-        [
-            queries_ref[:, (head * groups + g) * width : (head * groups + g + 1) * width]
-            for g in range(groups)
-        ],
-        axis=0,
-    )
-
-
 def padded_rows(rows):
     return jnp.concatenate(
         [rows, jnp.zeros((LANES - rows.shape[0], rows.shape[1]), rows.dtype)], axis=0
     )
 
 
+def score_kernel(
+    groups, chunk, queries_hbm, new_keys_hbm, key_hbm,
+    near_ref, far_hbm, fresh_ref,
+    queries_ref, new_keys_ref, keys_ref, far_ref, small_sems, key_sems, far_sems,
+):
+    page_count, page_tokens, _ = key_hbm.shape
+    resident, rows, tokens = near_ref.shape
+    kv_heads = fresh_ref.shape[0]
+    drafts = queries_hbm.shape[0]
+    width = LANES
+    scale = width ** (-0.5) * LOG2E
+    small = [
+        pltpu.make_async_copy(queries_hbm, queries_ref, small_sems.at[0]),
+        pltpu.make_async_copy(new_keys_hbm, new_keys_ref, small_sems.at[1]),
+    ]
+    for copy in small:
+        copy.start()
+    key_copies = []
+    for c in range(page_count // chunk):
+        pages = pl.ds(c * chunk, chunk)
+        copy = pltpu.make_async_copy(key_hbm.at[pages], keys_ref.at[pages], key_sems.at[c])
+        copy.start()
+        key_copies.append(copy)
+    for copy in small:
+        copy.wait()
+    contract = (((1,), (1,)), ((), ()))
+    query_heads = []
+    for h in range(kv_heads):
+        blocks = [
+            queries_ref[t : t + TILE, (h * groups + g) * width : (h * groups + g + 1) * width]
+            for t in range(0, drafts, TILE)
+            for g in range(groups)
+        ]
+        query_heads.append(jnp.concatenate(blocks, axis=0))
+        fresh_ref[h] = (
+            lax.dot_general(
+                query_heads[h], padded_rows(new_keys_ref[:, h * width : (h + 1) * width]),
+                contract, preferred_element_type=jnp.float32,
+            )
+            * scale
+        )
+    span = chunk * page_tokens
+    for c, copy in enumerate(key_copies):
+        copy.wait()
+        for h in range(kv_heads):
+            keys = keys_ref[c * chunk : (c + 1) * chunk, :, h * width : (h + 1) * width]
+            scores = lax.dot_general(
+                query_heads[h], keys.reshape(span, width), contract,
+                preferred_element_type=jnp.float32,
+            )
+            place = slice(c * span, (c + 1) * span)
+            if h < resident:
+                near_ref[h, :, place] = scores * scale
+            else:
+                far_ref[h - resident, :, place] = scores * scale
+    far_copies = []
+    for h in range(kv_heads - resident):
+        copy = pltpu.make_async_copy(far_ref.at[h], far_hbm.at[h], far_sems.at[h])
+        copy.start()
+        far_copies.append(copy)
+    for copy in far_copies:
+        copy.wait()
+
+
 def attend_kernel(
-    wanted_ref, queries_ref, keys_ref, values_ref, new_keys_ref, new_values_ref, out_ref
+    drafts, groups, wanted_ref, near_ref, far_hbm, fresh_ref, value_hbm, new_values_hbm,
+    out_ref,
+    values_ref, far_ref, new_values_ref, value_sems, far_sems, small_sem,
 ):
-    page_count, page_tokens, head_span = keys_ref.shape
-    tokens = page_count * page_tokens
-    kv_heads = wanted_ref.shape[1]
-    drafts = queries_ref.shape[0]
-    groups = queries_ref.shape[1] // head_span
-    rows = drafts * groups
+    page_count, page_tokens, _ = value_hbm.shape
+    resident, rows, tokens = near_ref.shape
+    kv_heads = fresh_ref.shape[0]
     devices, piece, width = out_ref.shape
     share = piece - STATS
     pieces = rows // share
-    scale = width ** (-0.5) * LOG2E
+    small = pltpu.make_async_copy(new_values_hbm, new_values_ref, small_sem)
+    value_copies = []
+    far_copies = []
+    for h in range(kv_heads):
+        heads = pl.ds(h * width, width)
+        copy = pltpu.make_async_copy(
+            value_hbm.at[:, :, heads], values_ref.at[h], value_sems.at[h]
+        )
+        copy.start()
+        value_copies.append(copy)
+        if h == 0:
+            small.start()
+        if h >= resident:
+            copy = pltpu.make_async_copy(
+                far_hbm.at[h - resident], far_ref.at[h - resident], far_sems.at[h - resident]
+            )
+            copy.start()
+            far_copies.append(copy)
     wanted = jnp.sum(wanted_ref[...], axis=0)
     bias = jnp.where(wanted > 0.5, 0.0, ABSENT)
     slot = lax.broadcasted_iota(jnp.int32, (LANES, tokens), 0)
@@ -72,22 +151,19 @@
     flags = jnp.where(wanted > 0.5, 1.0, 0.0).astype(jnp.bfloat16)
     token_flags = jnp.dot(flags, expand, preferred_element_type=jnp.float32)
     token_bias = jnp.where(token_flags > 0.5, 0.0, ABSENT)
-    position = lax.broadcasted_iota(jnp.int32, (rows, LANES), 0) % drafts
+    row = lax.broadcasted_iota(jnp.int32, (rows, LANES), 0)
     lane = lax.broadcasted_iota(jnp.int32, (rows, LANES), 1)
+    position = row // (groups * TILE) * TILE + row % TILE
     causal = jnp.where(lane <= position, 0.0, ABSENT)
     stats = jnp.zeros((rows, LANES), jnp.float32)
-    contract = (((1,), (1,)), ((), ()))
     for h in range(kv_heads):
-        span = slice(h * width, (h + 1) * width)
-        query_rows = head_queries(queries_ref, h, groups)
-        keys = keys_ref[:, :, span].reshape(tokens, width)
-        scores = lax.dot_general(query_rows, keys, contract, preferred_element_type=jnp.float32)
-        scores = scores * scale + token_bias[h : h + 1, :]
-        fresh = lax.dot_general(
-            query_rows, padded_rows(new_keys_ref[:, span]), contract,
-            preferred_element_type=jnp.float32,
-        )
-        fresh = fresh * scale + causal + bias[h : h + 1, page_count : page_count + 1]
+        if h >= resident:
+            far_copies[h - resident].wait()
+            scores = far_ref[h - resident]
+        else:
+            scores = near_ref[h]
+        scores = scores + token_bias[h : h + 1, :]
+        fresh = fresh_ref[h] + causal + bias[h : h + 1, page_count : page_count + 1]
         highest = jnp.maximum(
             jnp.max(scores, axis=1, keepdims=True), jnp.max(fresh, axis=1, keepdims=True)
         )
@@ -98,14 +174,18 @@
         totals = jnp.sum(weights.astype(jnp.float32), axis=1, keepdims=True) + jnp.sum(
             fresh_weights.astype(jnp.float32), axis=1, keepdims=True
         )
-        values = values_ref[:, :, span].reshape(tokens, width)
+        if h == 0:
+            small.wait()
+        value_copies[h].wait()
+        values = values_ref[h].reshape(tokens, width)
         weighted = jnp.dot(weights, values, preferred_element_type=jnp.float32)
         weighted = weighted + jnp.dot(
-            fresh_weights, padded_rows(new_values_ref[:, span]), preferred_element_type=jnp.float32
+            fresh_weights, padded_rows(new_values_ref[:, h * width : (h + 1) * width]),
+            preferred_element_type=jnp.float32,
         )
         weighted = weighted.astype(jnp.bfloat16)
         for i in range(pieces):
-            out_ref[h * pieces + i, :share, :] = weighted[i * share : (i + 1) * share]
+            out_ref[i * kv_heads + h, :share, :] = weighted[i * share : (i + 1) * share]
         coarse = totals.astype(jnp.bfloat16).astype(jnp.float32)
         level = jnp.where(present, offset, ABSENT)
         stats = jnp.where(lane == h * STATS, level, stats)
@@ -116,7 +196,7 @@
         part = turned if i == 0 else pltpu.roll(turned, LANES - i * share, 1)
         part = part.astype(jnp.bfloat16)
         for h in range(kv_heads):
-            out_ref[h * pieces + i, share:, :] = part[h * STATS : (h + 1) * STATS]
+            out_ref[i * kv_heads + h, share:, :] = part[h * STATS : (h + 1) * STATS]
 
 
 def merge_kernel(pieces_ref, out_ref):
@@ -153,17 +233,22 @@
 
 
 def on_device(queries, key_cache, value_cache, new_keys, new_values, chosen):
-    page_count, _, head_span = key_cache.shape
+    page_count, page_tokens, head_span = key_cache.shape
     kv_heads = chosen.shape[0]
     width = head_span // kv_heads
     drafts = queries.shape[0]
     groups = queries.shape[1] // head_span
     rows = drafts * groups
+    tokens = page_count * page_tokens
     devices = lax.axis_size("page")
     share = kv_heads * rows // devices
+    chunk = 4
+    resident = min(kv_heads - 1, RESIDENT_BYTES // (4 * rows * tokens))
+    distant = kv_heads - resident
     f32 = jnp.float32
     bf16 = jnp.bfloat16
-    limit = pltpu.CompilerParams(vmem_limit_bytes=24 * 1024 * 1024)
+    dma = pltpu.SemaphoreType.DMA
+    limit = pltpu.CompilerParams(vmem_limit_bytes=24 * 2**20)
 
     wanted = pl.pallas_call(
         lambda *refs: spread_kernel(page_count, *refs),
@@ -174,14 +259,50 @@
         name="spread",
     )(chosen)
     wanted = exchange(wanted)
+    near, far, fresh = pl.pallas_call(
+        lambda *refs: score_kernel(groups, chunk, *refs),
+        out_shape=(
+            pltpu.VMEM((resident, rows, tokens), f32),
+            pltpu.HBM((distant, rows, tokens), f32),
+            pltpu.VMEM((kv_heads, rows, LANES), f32),
+        ),
+        in_specs=[hbm()] * 3,
+        out_specs=(vmem(), hbm(), vmem()),
+        scratch_shapes=[
+            pltpu.VMEM(queries.shape, bf16),
+            pltpu.VMEM(new_keys.shape, bf16),
+            pltpu.VMEM(key_cache.shape, bf16),
+            pltpu.VMEM((distant, rows, tokens), f32),
+            dma((2,)),
+            dma((page_count // chunk,)),
+            dma((distant,)),
+        ],
+        compiler_params=limit,
+        cost_estimate=pl.CostEstimate(
+            flops=2 * kv_heads * rows * tokens * width,
+            bytes_accessed=2 * tokens * head_span,
+            transcendentals=0,
+        ),
+        name="scores",
+    )(*keep_in(pltpu.HBM, queries, new_keys, key_cache))
+    far, value_cache, new_values = keep_in(pltpu.HBM, far, value_cache, new_values)
+    wanted, near, fresh = keep_in(pltpu.VMEM, wanted, near, fresh)
     pieces = pl.pallas_call(
-        attend_kernel,
+        lambda *refs: attend_kernel(drafts, groups, *refs),
         out_shape=jax.ShapeDtypeStruct((devices, share + STATS, width), bf16),
-        in_specs=[vmem()] * 6,
+        in_specs=[vmem(), vmem(), hbm(), vmem(), hbm(), hbm()],
         out_specs=vmem(),
+        scratch_shapes=[
+            pltpu.VMEM((kv_heads, page_count, page_tokens, width), bf16),
+            pltpu.VMEM((distant, rows, tokens), f32),
+            pltpu.VMEM(new_values.shape, bf16),
+            dma((kv_heads,)),
+            dma((distant,)),
+            dma,
+        ],
         compiler_params=limit,
         name="attend",
-    )(wanted, queries, key_cache, value_cache, new_keys, new_values)
+    )(wanted, near, far, fresh, value_cache, new_values)
     pieces = exchange(pieces)
     finished = pl.pallas_call(
         merge_kernel,
@@ -193,8 +314,8 @@
     )(pieces)
     result = exchange(finished)
     return (
-        result.reshape(kv_heads * groups, drafts, width)
-        .transpose(1, 0, 2)
+        result.reshape(drafts // TILE, kv_heads * groups, TILE, width)
+        .transpose(0, 2, 1, 3)
         .reshape(drafts, kv_heads * groups * width)
     )
 

time: 49.3 us -> 46.6 us (0.945)
  blocking collectives: 35.6 us -> 23.5 us
  Pallas kernels: 5.1 us -> 12.8 us
  starting transfers between devices: 0 us -> 7.39 us
  local copies, waits for them, and re-layouts: 8.14 us -> 1.34 us
  waiting for transfers between devices: 0 us -> 1.31 us
    all_to_all x3 -> x2, blocking collectives: 35.6 us -> 23.5 us  [exchange(): lax.all_to_all(pieces, 'page', split_axis=0, concat_axis=0, tiled=True)]
    all_to_all x0 -> x1, starting transfers between devices: none -> 7.39 us  [exchange(): lax.all_to_all(pieces, 'page', split_axis=0, concat_axis=0, tiled=True)]
    pallas_call x1 -> x2, Pallas kernels: 4.18 us -> 11.2 us  [the longest x1 5.61 us: on_device(): pl.pallas_call(lambda *refs: attend_kernel(drafts, groups, *refs), out_sh...]
    unnamed x12 -> x3, local copies, waits for them, and re-layouts: 7.48 us -> 1.34 us
    all_to_all x0 -> x1, waiting for transfers between devices: none -> 1.31 us  [exchange(): lax.all_to_all(pieces, 'page', split_axis=0, concat_axis=0, tiled=True)]
    reshape x1 -> x0, local copies, waits for them, and re-layouts: 0.66 us -> none  [on_device(): return result.reshape(kv_heads * groups, drafts, width).transpose(1, 0, 2...]
    pallas_call x1, Pallas kernels: 0.3 us -> 0.93 us  [on_device(): pl.pallas_call(lambda *refs: spread_kernel(page_count, *refs), out_shape=...]
  transfers between devices with their start and end apart: 0 -> 1, of which waited for: 0 -> 1; matrix products, arithmetic and copies ran while one was open for 0% -> 0% of each run, Pallas kernels for 0% -> 12%
where the time goes in v2:
time: 46.6 us; the launch traced here: 46.3 us
  blocking collectives  23.5 us (50%)
  Pallas kernels  12.8 us (27%)
  starting transfers between devices  7.39 us (16%)
  local copies, waits for them, and re-layouts  1.34 us (3%)
  waiting for transfers between devices  1.31 us (3%)
    all_to_all x2, blocking collectives, exchange(): lax.all_to_all(pieces, 'page', split_axis=0, concat_axis=0, tiled=True)  23.5 us
    all_to_all x1, starting transfers between devices, exchange(): lax.all_to_all(pieces, 'page', split_axis=0, concat_axis=0, tiled=True)  7.39 us
    pallas_call x1, Pallas kernels, on_device(): pl.pallas_call(lambda *refs: attend_kernel(drafts, groups, *refs), out_sh...  5.61 us
    pallas_call x1, Pallas kernels, on_device(): pl.pallas_call(lambda *refs: score_kernel(groups, chunk, *refs), out_shap...  5.58 us
    unnamed x3, local copies, waits for them, and re-layouts  1.34 us
    all_to_all x1, waiting for transfers between devices, exchange(): lax.all_to_all(pieces, 'page', split_axis=0, concat_axis=0, tiled=True)  1.31 us
    pallas_call x1, Pallas kernels, on_device(): pl.pallas_call(lambda *refs: spread_kernel(page_count, *refs), out_shape=...  0.93 us
  transfers between devices with their start and end apart: 1, of which 1 were waited for; matrix products, arithmetic and copies ran while one was open for 0% of the time, Pallas kernels for 12%

profile of v2, /device:TPU:0, one launch (start us, length us, event | category | flops | bytes accessed | tf_op | source)
XLA Modules:
  0.0 46.3 jit_solution(9714165649591529790)
XLA Ops:
  0.0 0.0 copy-start
  0.0 0.7 %copy-done = s32[8,16]{1,0:T(8,128)S(1)} copy-done((s32[8,16]{1,0:T(8,128)S(1)}, s32[8,16]{1,0:T(8,128)}, u32[]{:S(2)}) %copy-start) | copy-done | bytes 536
  0.7 0.9 %spread.1 = f32[16,8,128]{2,1,0:T(8,128)} custom-call(s32[8,16]{1,0:T(8,128)S(1)} %copy-done), custom_call_target="tpu_custom_call" | custom-call | tf_op jit(solution)/shard_map/spread/pallas_call | solution.py:253
  1.6 7.4 %all-to-all-start = ((f32[16,8,128]{2,1,0:T(8,128)}), f32[16,8,128]{2,1,0:T(8,128)S(1)}, u32[]{:S(2)}, u32[]{:S(2)}) async-start(f32[16,8,128]{2,1,0:T(8,128)} %spread.1), calls=%async_computation | async-start | bytes 131072 | tf_op jit(solution)/shard_map/all_to_all | solution.py:232
  9.0 5.6 %scores.1 = (f32[6,64,2048]{2,1,0:T(8,128)S(1)}, f32[2,64,2048]{2,1,0:T(8,128)}, f32[8,64,128]{2,1,0:T(8,128)S(1)}) custom-call(bf16[16,4096]{1,0:T(8,128)(2,1)} %refs_0_.3, bf16[16,1024]{1,0:T(8,128)(2,1)} %refs_1_.1, bf16[32,64,1024]{2,1,0:T(8,128)(2,1)} %refs_2_.1), custom_call_target="tpu_custom_call" | custom-call | flops 268435456 | bytes 4194304 | tf_op jit(solution)/shard_map/scores/pallas_call | solution.py:262
  14.6 1.3 %all-to-all-done.refs_0_ = f32[16,8,128]{2,1,0:T(8,128)S(1)} async-done(((f32[16,8,128]{2,1,0:T(8,128)}), f32[16,8,128]{2,1,0:T(8,128)S(1)}, u32[]{:S(2)}, u32[]{:S(2)}) %all-to-all-start) | async-done | bytes 65568 | tf_op jit(solution)/shard_map/all_to_all | solution.py:232
  15.9 5.6 %attend.1 = bf16[16,40,128]{2,1,0:T(8,128)(2,1)S(1)} custom-call(f32[16,8,128]{2,1,0:T(8,128)S(1)} %all-to-all-done.refs_0_, f32[6,64,2048]{2,1,0:T(8,128)S(1)} %get-tuple-element.8.refs_1_, f32[2,64,2048]{2,1,0:T(8,128)} %get-tuple-element.9.refs_2_, f32[8,64,128]{2,1,0:T(8,128)S(1)} %get-tuple-element.10.refs_3_, bf16[32,64,1024]{2,1,0:T(8,128)(2,1)} %refs_4_.1, ...), custom_call_target="tpu_custom_call" | custom-call | tf_op jit(solution)/shard_map/attend/pallas_call | solution.py:290
  21.5 13.0 %all_to_all.15.pieces_ref = bf16[16,40,128]{2,1,0:T(8,128)(2,1)S(1)} all-to-all(bf16[16,40,128]{2,1,0:T(8,128)(2,1)S(1)} %attend.1), channel_id=1, replica_groups=mesh['grp'=2,'page'=16] {'page'}, dimensions={0} | all-to-all | bytes 327680 | tf_op jit(solution)/shard_map/all_to_all | solution.py:232
  34.5 0.6 %merge.1 = bf16[16,32,128]{2,1,0:T(8,128)(2,1)S(1)} custom-call(bf16[16,40,128]{2,1,0:T(8,128)(2,1)S(1)} %all_to_all.15.pieces_ref), custom_call_target="tpu_custom_call" | custom-call | tf_op jit(solution)/shard_map/merge/pallas_call | solution.py:307
  35.1 10.5 %all_to_all.16 = bf16[16,32,128]{2,1,0:T(8,128)(2,1)S(1)} all-to-all(bf16[16,32,128]{2,1,0:T(8,128)(2,1)S(1)} %merge.1), channel_id=1, replica_groups=mesh['grp'=2,'page'=16] {'page'}, dimensions={0} | all-to-all | bytes 262144 | tf_op jit(solution)/shard_map/all_to_all | solution.py:232
  45.6 0.7 %copy.8 = bf16[16,4096]{1,0:T(8,128)(2,1)} copy(bf16[16,4096]{1,0:T(8,128)(2,1)S(1)} %bitcast.5) | data formatting | bytes 262144
Async XLA Ops:
  0.0 0.7 %copy-start = (s32[8,16]{1,0:T(8,128)S(1)}, s32[8,16]{1,0:T(8,128)}, u32[]{:S(2)}) copy-start(s32[8,16]{1,0:T(8,128)} %refs_0_.2) | copy-start | bytes 1540
  1.6 14.3 %all-to-all-start = ((f32[16,8,128]{2,1,0:T(8,128)}), f32[16,8,128]{2,1,0:T(8,128)S(1)}, u32[]{:S(2)}, u32[]{:S(2)}) async-start(f32[16,8,128]{2,1,0:T(8,128)} %spread.1), calls=%async_computation | async-start | bytes 131072 | tf_op jit(solution)/shard_map/all_to_all | solution.py:232

commit v3 on v1

v3 whole, which is shorter than its diff:
```python
import jax
import jax.numpy as jnp
from jax import lax
from jax.experimental import pallas as pl
from jax.experimental.pallas import tpu as pltpu
from jax.sharding import PartitionSpec as P

ABSENT = -1e30
LOG2E = 1.4426950408889634
LANES = 128
STATS = 8
TILE = 8
PAIR = 2


def vmem():
    return pl.BlockSpec(memory_space=pltpu.VMEM)


def hbm():
    return pl.BlockSpec(memory_space=pltpu.HBM)


def keep_in(space, *arrays):
    return [pltpu.with_memory_space_constraint(array, space) for array in arrays]


def padded_rows(rows):
    return jnp.concatenate(
        [rows, jnp.zeros((LANES - rows.shape[0], rows.shape[1]), rows.dtype)], axis=0
    )


def token_copies(source_hbm, target_ref, sem, pair, span):
    copies = []
    for tile in range(source_hbm.shape[1]):
        copies.append(
            pltpu.make_async_copy(
                source_hbm.at[:, tile, :, pl.ds(pair * span, span)],
                target_ref.at[pair, tile], sem.at[pair],
            )
        )
    return copies


def wait_all(target_ref, sem, pair):
    pltpu.make_async_copy(target_ref.at[pair], target_ref.at[pair], sem.at[pair]).wait()


def score_kernel(
    groups, queries_hbm, new_keys_hbm, new_values_hbm, key_hbm,
    weights_ref, peaks_ref, new_values_ref,
    queries_ref, rows_ref, new_keys_ref, keys_ref, scores_ref, small_sems, key_sems,
):
    page_count, tiles, _, _ = key_hbm.shape
    kv_heads, rows, _ = weights_ref.shape
    drafts = queries_hbm.shape[0]
    width = LANES
    span = PAIR * width
    scale = width ** (-0.5) * LOG2E
    lanes = page_count * TILE
    tokens = tiles * lanes
    small = [
        pltpu.make_async_copy(queries_hbm, queries_ref, small_sems.at[0]),
        pltpu.make_async_copy(new_keys_hbm, new_keys_ref, small_sems.at[1]),
    ]
    for copy in small:
        copy.start()
    pl.delay(16)
    for p in range(kv_heads // PAIR):
        for copy in token_copies(key_hbm, keys_ref, key_sems, p, span):
            copy.start()
    late = pltpu.make_async_copy(new_values_hbm, new_values_ref, small_sems.at[2])
    for copy in small:
        copy.wait()
    late.start()
    contract = (((1,), (1,)), ((), ()))
    row = lax.broadcasted_iota(jnp.int32, (rows, LANES), 0)
    column = lax.broadcasted_iota(jnp.int32, (rows, LANES), 1)
    causal = column <= row // (groups * TILE) * TILE + row % TILE
    for h in range(kv_heads):
        blocks = [
            queries_ref[t : t + TILE, (h * groups + g) * width : (h * groups + g + 1) * width]
            for t in range(0, drafts, TILE)
            for g in range(groups)
        ]
        query_rows = jnp.concatenate(blocks, axis=0)
        rows_ref[h] = query_rows
        fresh = scale * lax.dot_general(
            query_rows, padded_rows(new_keys_ref[:, h * width : (h + 1) * width]), contract,
            preferred_element_type=jnp.float32,
        )
        fresh = jnp.where(causal, fresh, ABSENT)
        peak = jnp.max(fresh, axis=1, keepdims=True)
        weights_ref[h, :, tokens:] = jnp.exp2(fresh - peak).astype(jnp.bfloat16)
        peaks_ref[h, :, lanes:] = jnp.broadcast_to(peak, (rows, LANES))

    lane = lax.broadcasted_iota(jnp.int32, (rows, lanes), 1)

    def score(h):
        query_rows = rows_ref[h]
        for tile in range(tiles):
            keys = keys_ref[h // PAIR, tile, :, :, h % PAIR * width : (h % PAIR + 1) * width]
            scores_ref[h, :, tile * lanes : (tile + 1) * lanes] = lax.dot_general(
                query_rows, keys.reshape(lanes, width), contract,
                preferred_element_type=jnp.float32,
            )

    def weigh(h):
        peak = scores_ref[h, :, :lanes]
        for tile in range(1, tiles):
            peak = jnp.maximum(peak, scores_ref[h, :, tile * lanes : (tile + 1) * lanes])
        step = 1
        while step < TILE:
            ahead = pltpu.roll(peak, lanes - step, 1)
            behind = pltpu.roll(peak, step, 1)
            peak = jnp.maximum(peak, jnp.where(lane // step % 2 == 0, ahead, behind))
            step *= 2
        peaks_ref[h, :, :lanes] = peak * scale
        for tile in range(tiles):
            place = slice(tile * lanes, (tile + 1) * lanes)
            weights = jnp.exp2((scores_ref[h, :, place] - peak) * scale)
            weights_ref[h, :, place] = weights.astype(jnp.bfloat16)

    for p in range(kv_heads // PAIR):
        wait_all(keys_ref, key_sems, p)
        for k in range(PAIR):
            score(p * PAIR + k)
            if p > 0:
                weigh((p - 1) * PAIR + k)
    late.wait()
    for k in range(PAIR):
        weigh(kv_heads - PAIR + k)


def attend_kernel(
    listed, me_ref, chosen_ref, weights_ref, peaks_ref, new_values_ref, value_hbm,
    out_ref,
    values_ref, scaled_ref, bias_ref, value_sems,
):
    page_count, tiles, _, _ = value_hbm.shape
    kv_heads, rows, _ = weights_ref.shape
    devices, piece, width = out_ref.shape
    share = piece - STATS
    pieces = rows // share
    span = PAIR * width
    pairs = kv_heads // PAIR
    lanes = page_count * TILE
    tokens = tiles * lanes
    for p in range(pairs):
        for copy in token_copies(value_hbm, values_ref, value_sems, p, span):
            copy.start()
    me = me_ref[0]
    target = me * page_count + lax.broadcasted_iota(jnp.int32, (kv_heads, lanes), 1) // TILE
    picked = target < 0
    for d in range(devices):
        chosen = chosen_ref[d]
        for j in range(listed):
            column = jnp.broadcast_to(chosen[:, j : j + 1], (kv_heads, lanes))
            picked = jnp.logical_or(picked, column == target)
    bias_ref[:, :lanes] = jnp.where(picked, 0.0, ABSENT)
    bias_ref[:, lanes:] = jnp.full((kv_heads, LANES), jnp.where(me == 0, 0.0, ABSENT))
    column = lax.broadcasted_iota(jnp.int32, (rows, LANES), 1)
    stats = [jnp.zeros((rows, LANES), jnp.float32)]

    def scale_head(h):
        level = peaks_ref[h] + bias_ref[h : h + 1, :]
        highest = jnp.max(level, axis=1, keepdims=True)
        present = highest > 0.5 * ABSENT
        factor = jnp.exp2(level - jnp.where(present, highest, 0.0)).astype(jnp.bfloat16)
        scaled = weights_ref[h, :, tokens:] * factor[:, lanes:]
        scaled_ref[h, :, tokens:] = scaled
        sums = scaled.astype(jnp.float32)
        for tile in range(tiles):
            place = slice(tile * lanes, (tile + 1) * lanes)
            scaled = weights_ref[h, :, place] * factor[:, :lanes]
            scaled_ref[h, :, place] = scaled
            scaled = scaled.astype(jnp.float32)
            for i in range(0, lanes, LANES):
                sums = sums + scaled[:, i : i + LANES]
        totals = jnp.sum(sums, axis=1, keepdims=True)
        top = jnp.where(present, highest, ABSENT)
        rest = [top, top, top, totals, totals]
        for k in range(5):
            part = rest[k].astype(jnp.bfloat16).astype(jnp.float32)
            stats[0] = jnp.where(column == h * STATS + k, part, stats[0])
            for later in range(k + 1, 3 if k < 3 else 5):
                rest[later] = rest[later] - part

    def product(p):
        values = values_ref[p].reshape(tokens, span)
        new_values = padded_rows(new_values_ref[:, p * span : (p + 1) * span])
        weights = scaled_ref[p * PAIR : (p + 1) * PAIR].reshape(PAIR * rows, tokens + LANES)
        half = tokens // 2
        weighted = jnp.dot(
            weights[:, :half], values[:half], preferred_element_type=jnp.float32
        ) + jnp.dot(
            weights[:, half:], jnp.concatenate([values[half:], new_values], axis=0),
            preferred_element_type=jnp.float32,
        )
        for k in range(PAIR):
            for i in range(pieces):
                first_row = k * rows + i * share
                out_ref[i * kv_heads + p * PAIR + k, :share, :] = weighted[
                    first_row : first_row + share, k * width : (k + 1) * width
                ].astype(jnp.bfloat16)

    for h in range(2 * PAIR):
        scale_head(h)
    for p in range(pairs):
        wait_all(values_ref, value_sems, p)
        product(p)
        if p + 2 < pairs:
            for k in range(PAIR):
                scale_head((p + 2) * PAIR + k)
    turned = padded_rows(stats[0]).T
    for i in range(pieces):
        part = turned if i == 0 else pltpu.roll(turned, LANES - i * share, 1)
        part = part.astype(jnp.bfloat16)
        for h in range(kv_heads):
            out_ref[i * kv_heads + h, share:, :] = part[h * STATS : (h + 1) * STATS]


def merge_kernel(pieces_ref, out_ref):
    devices, piece, width = pieces_ref.shape
    share = piece - STATS
    stats = jnp.concatenate(
        [pieces_ref[d, share:, :].astype(jnp.float32) for d in range(devices)], axis=0
    )
    if devices * STATS < LANES:
        stats = jnp.concatenate(
            [stats, jnp.zeros((LANES - devices * STATS, width), jnp.float32)], axis=0
        )
    turned = stats.T[:share]
    def stat(d, k):
        return turned[:, d * STATS + k : d * STATS + k + 1]

    levels = [stat(d, 0) + (stat(d, 1) + stat(d, 2)) for d in range(devices)]
    highest = levels[0]
    for level in levels[1:]:
        highest = jnp.maximum(highest, level)
    totals = jnp.zeros((share, 1), jnp.float32)
    weighted = jnp.zeros((share, width), jnp.float32)
    for d in range(devices):
        factor = jnp.exp2(levels[d] - highest)
        totals = totals + (stat(d, 3) + stat(d, 4)) * factor
        weighted = weighted + pieces_ref[d, :share, :].astype(jnp.float32) * factor
    finished = (weighted / totals).astype(jnp.bfloat16)
    for d in range(devices):
        out_ref[d] = finished


def exchange(pieces):
    return lax.all_to_all(pieces, "page", split_axis=0, concat_axis=0, tiled=True)


def on_device(queries, key_cache, value_cache, new_keys, new_values, chosen):
    page_count, page_tokens, head_span = key_cache.shape
    kv_heads, listed = chosen.shape
    width = head_span // kv_heads
    drafts = queries.shape[0]
    groups = queries.shape[1] // head_span
    rows = drafts * groups
    tokens = page_count * page_tokens
    tiles = page_tokens // TILE
    lanes = page_count * TILE
    pairs = kv_heads // PAIR
    span = PAIR * width
    devices = lax.axis_size("page")
    share = kv_heads * rows // devices
    f32 = jnp.float32
    bf16 = jnp.bfloat16
    dma = pltpu.SemaphoreType.DMA
    limit = pltpu.CompilerParams(vmem_limit_bytes=24 * 2**20)
    key_cache = key_cache.reshape(page_count, tiles, TILE, head_span)
    value_cache = value_cache.reshape(page_count, tiles, TILE, head_span)

    me = lax.axis_index("page").astype(jnp.int32).reshape(1)
    listing = jnp.pad(chosen, ((0, 0), (0, LANES - listed)), constant_values=-1)
    chosen_all = exchange(jnp.broadcast_to(listing[None], (devices,) + listing.shape))
    weights, peaks, new_values = pl.pallas_call(
        lambda *refs: score_kernel(groups, *refs),
        out_shape=(
            pltpu.VMEM((kv_heads, rows, tokens + LANES), bf16),
            pltpu.VMEM((kv_heads, rows, lanes + LANES), f32),
            pltpu.VMEM(new_values.shape, bf16),
        ),
        in_specs=[hbm()] * 4,
        out_specs=(vmem(), vmem(), vmem()),
        scratch_shapes=[
            pltpu.VMEM(queries.shape, bf16),
            pltpu.VMEM((kv_heads, rows, width), bf16),
            pltpu.VMEM(new_keys.shape, bf16),
            pltpu.VMEM((pairs, tiles, page_count, TILE, span), bf16),
            pltpu.VMEM((kv_heads, rows, tokens), f32),
            dma((3,)),
            dma((pairs,)),
        ],
        compiler_params=limit,
        cost_estimate=pl.CostEstimate(
            flops=2 * kv_heads * rows * tokens * width,
            bytes_accessed=2 * tokens * head_span,
            transcendentals=0,
        ),
        name="scores",
    )(*keep_in(pltpu.HBM, queries, new_keys, new_values, key_cache))
    value_cache, = keep_in(pltpu.HBM, value_cache)
    resting = keep_in(pltpu.VMEM, chosen_all, weights, peaks, new_values)
    pieces = pl.pallas_call(
        lambda *refs: attend_kernel(listed, *refs),
        out_shape=jax.ShapeDtypeStruct((devices, share + STATS, width), bf16),
        in_specs=[pl.BlockSpec(memory_space=pltpu.SMEM)] + [vmem()] * 4 + [hbm()],
        out_specs=vmem(),
        scratch_shapes=[
            pltpu.VMEM((pairs, tiles, page_count, TILE, span), bf16),
            pltpu.VMEM((kv_heads, rows, tokens + LANES), bf16),
            pltpu.VMEM((kv_heads, lanes + LANES), f32),
            dma((pairs,)),
        ],
        compiler_params=limit,
        name="attend",
    )(me, *resting, value_cache)
    pieces = exchange(pieces)
    finished = pl.pallas_call(
        merge_kernel,
        out_shape=jax.ShapeDtypeStruct((devices, share, width), bf16),
        in_specs=[vmem()],
        out_specs=vmem(),
        compiler_params=limit,
        name="merge",
    )(pieces)
    result = exchange(finished)
    return (
        result.reshape(drafts // TILE, kv_heads * groups, TILE, width)
        .transpose(0, 2, 1, 3)
        .reshape(drafts, kv_heads * groups * width)
    )


def solution(mesh):
    placed = (
        P("grp", None),
        P(("grp", "page"), None, None),
        P(("grp", "page"), None, None),
        P("grp", None),
        P("grp", None),
        P("grp", "page"),
    )
    return jax.shard_map(
        on_device, mesh=mesh, in_specs=placed, out_specs=P("grp", None), check_vma=False
    )
```

time: 49.3 us -> 43 us (0.87)
  blocking collectives: 35.6 us -> 22.1 us
  starting transfers between devices: 0 us -> 7.39 us
  local copies, waits for them, and re-layouts: 8.14 us -> 1.98 us
  Pallas kernels: 5.1 us -> 8.54 us
  waiting for transfers between devices: 0 us -> 2.63 us
    all_to_all x3 -> x2, blocking collectives: 35.6 us -> 22.1 us  [exchange(): lax.all_to_all(pieces, 'page', split_axis=0, concat_axis=0, tiled=True)]
    all_to_all x0 -> x1, starting transfers between devices: none -> 7.39 us  [exchange(): lax.all_to_all(pieces, 'page', split_axis=0, concat_axis=0, tiled=True)]
    unnamed x12 -> x1, local copies, waits for them, and re-layouts: 7.48 us -> 0.66 us
    pallas_call x2, Pallas kernels: 4.48 us -> 7.79 us  [the longest x1 4.25 us: on_device(): pl.pallas_call(lambda *refs: score_kernel(groups, *refs), out_shape=(pltp...]
    all_to_all x0 -> x1, waiting for transfers between devices: none -> 2.63 us  [exchange(): lax.all_to_all(pieces, 'page', split_axis=0, concat_axis=0, tiled=True)]
    pad x0 -> x1, local copies, waits for them, and re-layouts: none -> 0.69 us  [on_device(): listing = jnp.pad(chosen, ((0, 0), (0, LANES - listed)), constant_values=-1)]
    reshape x1 -> x0, local copies, waits for them, and re-layouts: 0.66 us -> none  [on_device(): return result.reshape(kv_heads * groups, drafts, width).transpose(1, 0, 2...]
    broadcast_in_dim x0 -> x1, local copies, waits for them, and re-layouts: none -> 0.64 us  [on_device(): jnp.broadcast_to(listing[None], (devices,) + listing.shape)]
  transfers between devices with their start and end apart: 0 -> 1, of which waited for: 0 -> 1; matrix products, arithmetic and copies ran while one was open for 0% -> 0% of each run, Pallas kernels for 0% -> 10%
where the time goes in v3:
time: 43 us; the launch traced here: 42.7 us
  blocking collectives  22.1 us (51%)
  Pallas kernels  8.54 us (20%)
  starting transfers between devices  7.39 us (17%)
  waiting for transfers between devices  2.63 us (6%)
  local copies, waits for them, and re-layouts  1.98 us (5%)
    all_to_all x2, blocking collectives, exchange(): lax.all_to_all(pieces, 'page', split_axis=0, concat_axis=0, tiled=True)  22.1 us
    all_to_all x1, starting transfers between devices, exchange(): lax.all_to_all(pieces, 'page', split_axis=0, concat_axis=0, tiled=True)  7.39 us
    pallas_call x1, Pallas kernels, on_device(): pl.pallas_call(lambda *refs: score_kernel(groups, *refs), out_shape=(pltp...  4.25 us
    pallas_call x1, Pallas kernels, on_device(): pl.pallas_call(lambda *refs: attend_kernel(listed, *refs), out_shape=jax....  3.54 us
    all_to_all x1, waiting for transfers between devices, exchange(): lax.all_to_all(pieces, 'page', split_axis=0, concat_axis=0, tiled=True)  2.63 us
  transfers between devices with their start and end apart: 1, of which 1 were waited for; matrix products, arithmetic and copies ran while one was open for 0% of the time, Pallas kernels for 10%

profile of v3, /device:TPU:0, one launch (start us, length us, event | category | flops | bytes accessed | tf_op | source)
XLA Modules:
  0.0 42.7 jit_solution(11773421540473700521)
XLA Ops:
  0.0 0.7 %pad.4 = s32[8,128]{1,0:T(8,128)S(1)} pad(s32[8,16]{1,0:T(8,128)} %param.11, s32[]{:T(128)} %constant.1.clone.1), padding=0_0x0_112 | pad | bytes 4612 | tf_op jit(solution)/shard_map/jit(_pad)/pad | solution.py:279
  0.7 0.6 %broadcast_in_dim.2 = s32[16,8,128]{2,1,0:T(8,128)} broadcast(s32[8,128]{1,0:T(8,128)S(1)} %pad.4), dimensions={1,2} | broadcast | bytes 69632 | tf_op jit(solution)/shard_map/broadcast_in_dim | solution.py:280
  1.3 7.4 %all-to-all-start = ((s32[16,8,128]{2,1,0:T(8,128)}), s32[16,8,128]{2,1,0:T(8,128)S(1)}, u32[]{:S(2)}, u32[]{:S(2)}) async-start(s32[16,8,128]{2,1,0:T(8,128)} %broadcast_in_dim.2), calls=%async_computation | async-start | bytes 131072 | tf_op jit(solution)/shard_map/all_to_all | solution.py:254
  8.7 4.3 %scores.1 = (bf16[8,64,2176]{2,1,0:T(8,128)(2,1)S(1)}, f32[8,64,384]{2,1,0:T(8,128)S(1)}, bf16[16,1024]{1,0:T(8,128)(2,1)S(1)}) custom-call(bf16[16,4096]{1,0:T(8,128)(2,1)} %refs_0_.1, bf16[16,1024]{1,0:T(8,128)(2,1)} %refs_1_.1, bf16[16,1024]{1,0:T(8,128)(2,1)} %refs_2_.1, bf16[32,8,8,1024]{3,2,1,0:T(8,128)(2,1)} %bitcast.8), custom_call_target="tpu_custom_call" | custom-call | flops 268435456 | bytes 4194304 | tf_op jit(solution)/shard_map/scores/pallas_call | solution.py:281
  13.0 2.6 %all-to-all-done.refs_1_ = s32[16,8,128]{2,1,0:T(8,128)S(1)} async-done(((s32[16,8,128]{2,1,0:T(8,128)}), s32[16,8,128]{2,1,0:T(8,128)S(1)}, u32[]{:S(2)}, u32[]{:S(2)}) %all-to-all-start) | async-done | bytes 65568 | tf_op jit(solution)/shard_map/all_to_all | solution.py:254
  15.6 3.5 %attend.1 = bf16[16,40,128]{2,1,0:T(8,128)(2,1)S(1)} custom-call(s32[1]{0:T(128)} %bitcast.refs_0_, s32[16,8,128]{2,1,0:T(8,128)S(1)} %all-to-all-done.refs_1_, bf16[8,64,2176]{2,1,0:T(8,128)(2,1)S(1)} %get-tuple-element.8.refs_2_, f32[8,64,384]{2,1,0:T(8,128)S(1)} %get-tuple-element.9.refs_3_, bf16[16,1024]{1,0:T(8,128)(2,1)S(1)} %get-tuple-element.10.refs_4_, ...), custom_call_target="tpu_custom_call" | custom-call | tf_op jit(solution)/shard_map/attend/pallas_call | solution.py:309
  19.2 11.6 %all_to_all.15.pieces_ref = bf16[16,40,128]{2,1,0:T(8,128)(2,1)S(1)} all-to-all(bf16[16,40,128]{2,1,0:T(8,128)(2,1)S(1)} %attend.1), channel_id=1, replica_groups=mesh['grp'=2,'page'=16] {'page'}, dimensions={0} | all-to-all | bytes 327680 | tf_op jit(solution)/shard_map/all_to_all | solution.py:254
  30.8 0.8 %merge.1 = bf16[16,32,128]{2,1,0:T(8,128)(2,1)S(1)} custom-call(bf16[16,40,128]{2,1,0:T(8,128)(2,1)S(1)} %all_to_all.15.pieces_ref), custom_call_target="tpu_custom_call" | custom-call | tf_op jit(solution)/shard_map/merge/pallas_call | solution.py:324
  31.5 10.5 %all_to_all.16 = bf16[16,32,128]{2,1,0:T(8,128)(2,1)S(1)} all-to-all(bf16[16,32,128]{2,1,0:T(8,128)(2,1)S(1)} %merge.1), channel_id=1, replica_groups=mesh['grp'=2,'page'=16] {'page'}, dimensions={0} | all-to-all | bytes 262144 | tf_op jit(solution)/shard_map/all_to_all | solution.py:254
  42.0 0.7 %copy.8 = bf16[16,4096]{1,0:T(8,128)(2,1)} copy(bf16[16,4096]{1,0:T(8,128)(2,1)S(1)} %bitcast.10) | data formatting | bytes 262144
Async XLA Ops:
  1.3 14.3 %all-to-all-start = ((s32[16,8,128]{2,1,0:T(8,128)}), s32[16,8,128]{2,1,0:T(8,128)S(1)}, u32[]{:S(2)}, u32[]{:S(2)}) async-start(s32[16,8,128]{2,1,0:T(8,128)} %broadcast_in_dim.2), calls=%async_computation | async-start | bytes 131072 | tf_op jit(solution)/shard_map/all_to_all | solution.py:254

commit v4 on v3

--- a/solution.py
+++ b/solution.py
@@ -99,17 +99,19 @@
 
     def score(h):
         query_rows = rows_ref[h]
+        peak = None
         for tile in range(tiles):
             keys = keys_ref[h // PAIR, tile, :, :, h % PAIR * width : (h % PAIR + 1) * width]
-            scores_ref[h, :, tile * lanes : (tile + 1) * lanes] = lax.dot_general(
+            scores = lax.dot_general(
                 query_rows, keys.reshape(lanes, width), contract,
                 preferred_element_type=jnp.float32,
             )
+            scores_ref[h, :, tile * lanes : (tile + 1) * lanes] = scores
+            peak = scores if peak is None else jnp.maximum(peak, scores)
+        peaks_ref[h, :, :lanes] = peak
 
     def weigh(h):
-        peak = scores_ref[h, :, :lanes]
-        for tile in range(1, tiles):
-            peak = jnp.maximum(peak, scores_ref[h, :, tile * lanes : (tile + 1) * lanes])
+        peak = peaks_ref[h, :, :lanes]
         step = 1
         while step < TILE:
             ahead = pltpu.roll(peak, lanes - step, 1)
@@ -207,12 +209,14 @@
 
     for h in range(2 * PAIR):
         scale_head(h)
-    for p in range(pairs):
-        wait_all(values_ref, value_sems, p)
-        product(p)
-        if p + 2 < pairs:
-            for k in range(PAIR):
-                scale_head((p + 2) * PAIR + k)
+    for p in range(0, pairs, 2):
+        both = range(p, min(p + 2, pairs))
+        for q in both:
+            wait_all(values_ref, value_sems, q)
+        for q in both:
+            product(q)
+        for h in range((p + 2) * PAIR, min((p + 4) * PAIR, kv_heads)):
+            scale_head(h)
     turned = padded_rows(stats[0]).T
     for i in range(pieces):
         part = turned if i == 0 else pltpu.roll(turned, LANES - i * share, 1)
@@ -224,28 +228,19 @@
 def merge_kernel(pieces_ref, out_ref):
     devices, piece, width = pieces_ref.shape
     share = piece - STATS
-    stats = jnp.concatenate(
-        [pieces_ref[d, share:, :].astype(jnp.float32) for d in range(devices)], axis=0
-    )
-    if devices * STATS < LANES:
-        stats = jnp.concatenate(
-            [stats, jnp.zeros((LANES - devices * STATS, width), jnp.float32)], axis=0
-        )
-    turned = stats.T[:share]
-    def stat(d, k):
-        return turned[:, d * STATS + k : d * STATS + k + 1]
-
-    levels = [stat(d, 0) + (stat(d, 1) + stat(d, 2)) for d in range(devices)]
-    highest = levels[0]
-    for level in levels[1:]:
-        highest = jnp.maximum(highest, level)
-    totals = jnp.zeros((share, 1), jnp.float32)
+
+    def stat(k):
+        return pieces_ref[:, share + k, :].astype(jnp.float32)
+
+    level = stat(0) + (stat(1) + stat(2))
+    factor = jnp.exp2(level - jnp.max(level, axis=0, keepdims=True))
+    totals = jnp.sum((stat(3) + stat(4)) * factor, axis=0, keepdims=True)
+    factor = factor / jnp.where(totals > 0.0, totals, 1.0)
+    turned = padded_rows(factor).T[:share] if devices < LANES else factor.T[:share]
     weighted = jnp.zeros((share, width), jnp.float32)
     for d in range(devices):
-        factor = jnp.exp2(levels[d] - highest)
-        totals = totals + (stat(d, 3) + stat(d, 4)) * factor
-        weighted = weighted + pieces_ref[d, :share, :].astype(jnp.float32) * factor
-    finished = (weighted / totals).astype(jnp.bfloat16)
+        weighted = weighted + pieces_ref[d, :share, :].astype(jnp.float32) * turned[:, d : d + 1]
+    finished = weighted.astype(jnp.bfloat16)
     for d in range(devices):
         out_ref[d] = finished
 

time: 43 us -> 42.2 us (0.981)
  Pallas kernels: 8.54 us -> 7.73 us
    pallas_call x1, Pallas kernels: 0.75 us -> 0.31 us  [on_device(): pl.pallas_call(merge_kernel, out_shape=jax.ShapeDtypeStruct((devices, sha...]
where the time goes in v4:
time: 42.2 us; the launch traced here: 41.9 us
  blocking collectives  22.1 us (52%)
  Pallas kernels  7.73 us (18%)
  starting transfers between devices  7.39 us (18%)
  waiting for transfers between devices  2.66 us (6%)
  local copies, waits for them, and re-layouts  1.98 us (5%)
    all_to_all x2, blocking collectives, exchange(): lax.all_to_all(pieces, 'page', split_axis=0, concat_axis=0, tiled=True)  22.1 us
    all_to_all x1, starting transfers between devices, exchange(): lax.all_to_all(pieces, 'page', split_axis=0, concat_axis=0, tiled=True)  7.39 us
    pallas_call x1, Pallas kernels, on_device(): pl.pallas_call(lambda *refs: score_kernel(groups, *refs), out_shape=(pltp...  4.22 us
    pallas_call x1, Pallas kernels, on_device(): pl.pallas_call(lambda *refs: attend_kernel(listed, *refs), out_shape=jax....  3.2 us
    all_to_all x1, waiting for transfers between devices, exchange(): lax.all_to_all(pieces, 'page', split_axis=0, concat_axis=0, tiled=True)  2.66 us
  transfers between devices with their start and end apart: 1, of which 1 were waited for; matrix products, arithmetic and copies ran while one was open for 0% of the time, Pallas kernels for 10%

profile of v4, /device:TPU:0, one launch (start us, length us, event | category | flops | bytes accessed | tf_op | source)
XLA Modules:
  0.0 41.9 jit_solution(12261600720750902989)
XLA Ops:
  0.0 0.7 %pad.4 = s32[8,128]{1,0:T(8,128)S(1)} pad(s32[8,16]{1,0:T(8,128)} %param.11, s32[]{:T(128)} %constant.1.clone.1), padding=0_0x0_112 | pad | bytes 4612 | tf_op jit(solution)/shard_map/jit(_pad)/pad | solution.py:274
  0.7 0.6 %broadcast_in_dim.2 = s32[16,8,128]{2,1,0:T(8,128)} broadcast(s32[8,128]{1,0:T(8,128)S(1)} %pad.4), dimensions={1,2} | broadcast | bytes 69632 | tf_op jit(solution)/shard_map/broadcast_in_dim | solution.py:275
  1.3 7.4 %all-to-all-start = ((s32[16,8,128]{2,1,0:T(8,128)}), s32[16,8,128]{2,1,0:T(8,128)S(1)}, u32[]{:S(2)}, u32[]{:S(2)}) async-start(s32[16,8,128]{2,1,0:T(8,128)} %broadcast_in_dim.2), calls=%async_computation | async-start | bytes 131072 | tf_op jit(solution)/shard_map/all_to_all | solution.py:249
  8.7 4.2 %scores.1 = (bf16[8,64,2176]{2,1,0:T(8,128)(2,1)S(1)}, f32[8,64,384]{2,1,0:T(8,128)S(1)}, bf16[16,1024]{1,0:T(8,128)(2,1)S(1)}) custom-call(bf16[16,4096]{1,0:T(8,128)(2,1)} %refs_0_.1, bf16[16,1024]{1,0:T(8,128)(2,1)} %refs_1_.1, bf16[16,1024]{1,0:T(8,128)(2,1)} %refs_2_.1, bf16[32,8,8,1024]{3,2,1,0:T(8,128)(2,1)} %bitcast.8), custom_call_target="tpu_custom_call" | custom-call | flops 268435456 | bytes 4194304 | tf_op jit(solution)/shard_map/scores/pallas_call | solution.py:276
  13.0 2.7 %all-to-all-done.refs_1_ = s32[16,8,128]{2,1,0:T(8,128)S(1)} async-done(((s32[16,8,128]{2,1,0:T(8,128)}), s32[16,8,128]{2,1,0:T(8,128)S(1)}, u32[]{:S(2)}, u32[]{:S(2)}) %all-to-all-start) | async-done | bytes 65568 | tf_op jit(solution)/shard_map/all_to_all | solution.py:249
  15.6 3.2 %attend.1 = bf16[16,40,128]{2,1,0:T(8,128)(2,1)S(1)} custom-call(s32[1]{0:T(128)} %bitcast.refs_0_, s32[16,8,128]{2,1,0:T(8,128)S(1)} %all-to-all-done.refs_1_, bf16[8,64,2176]{2,1,0:T(8,128)(2,1)S(1)} %get-tuple-element.8.refs_2_, f32[8,64,384]{2,1,0:T(8,128)S(1)} %get-tuple-element.9.refs_3_, bf16[16,1024]{1,0:T(8,128)(2,1)S(1)} %get-tuple-element.10.refs_4_, ...), custom_call_target="tpu_custom_call" | custom-call | tf_op jit(solution)/shard_map/attend/pallas_call | solution.py:304
  18.8 11.6 %all_to_all.15.pieces_ref = bf16[16,40,128]{2,1,0:T(8,128)(2,1)S(1)} all-to-all(bf16[16,40,128]{2,1,0:T(8,128)(2,1)S(1)} %attend.1), channel_id=1, replica_groups=mesh['grp'=2,'page'=16] {'page'}, dimensions={0} | all-to-all | bytes 327680 | tf_op jit(solution)/shard_map/all_to_all | solution.py:249
  30.4 0.3 merge.1
  30.7 10.5 %all_to_all.16 = bf16[16,32,128]{2,1,0:T(8,128)(2,1)S(1)} all-to-all(bf16[16,32,128]{2,1,0:T(8,128)(2,1)S(1)} %merge.1), channel_id=1, replica_groups=mesh['grp'=2,'page'=16] {'page'}, dimensions={0} | all-to-all | bytes 262144 | tf_op jit(solution)/shard_map/all_to_all | solution.py:249
  41.2 0.7 %copy.8 = bf16[16,4096]{1,0:T(8,128)(2,1)} copy(bf16[16,4096]{1,0:T(8,128)(2,1)S(1)} %bitcast.10) | data formatting | bytes 262144
Async XLA Ops:
  1.3 14.3 %all-to-all-start = ((s32[16,8,128]{2,1,0:T(8,128)}), s32[16,8,128]{2,1,0:T(8,128)S(1)}, u32[]{:S(2)}, u32[]{:S(2)}) async-start(s32[16,8,128]{2,1,0:T(8,128)} %broadcast_in_dim.2), calls=%async_computation | async-start | bytes 131072 | tf_op jit(solution)/shard_map/all_to_all | solution.py:249

commit v5 on v4

--- a/solution.py
+++ b/solution.py
@@ -45,6 +45,12 @@
 
 def wait_all(target_ref, sem, pair):
     pltpu.make_async_copy(target_ref.at[pair], target_ref.at[pair], sem.at[pair]).wait()
+
+
+def wait_part(target_ref, sem, pair, part):
+    half = target_ref.shape[1] // 2
+    place = target_ref.at[pair, pl.ds(part * half, half)]
+    pltpu.make_async_copy(place, place, sem.at[2 * pair + part]).wait()
 
 
 def score_kernel(
@@ -95,8 +101,6 @@
         weights_ref[h, :, tokens:] = jnp.exp2(fresh - peak).astype(jnp.bfloat16)
         peaks_ref[h, :, lanes:] = jnp.broadcast_to(peak, (rows, LANES))
 
-    lane = lax.broadcasted_iota(jnp.int32, (rows, lanes), 1)
-
     def score(h):
         query_rows = rows_ref[h]
         peak = None
@@ -112,12 +116,6 @@
 
     def weigh(h):
         peak = peaks_ref[h, :, :lanes]
-        step = 1
-        while step < TILE:
-            ahead = pltpu.roll(peak, lanes - step, 1)
-            behind = pltpu.roll(peak, step, 1)
-            peak = jnp.maximum(peak, jnp.where(lane // step % 2 == 0, ahead, behind))
-            step *= 2
         peaks_ref[h, :, :lanes] = peak * scale
         for tile in range(tiles):
             place = slice(tile * lanes, (tile + 1) * lanes)
@@ -138,7 +136,7 @@
 def attend_kernel(
     listed, me_ref, chosen_ref, weights_ref, peaks_ref, new_values_ref, value_hbm,
     out_ref,
-    values_ref, scaled_ref, bias_ref, value_sems,
+    values_ref, scaled_ref, bias_ref, sums_ref, value_sems,
 ):
     page_count, tiles, _, _ = value_hbm.shape
     kv_heads, rows, _ = weights_ref.shape
@@ -149,9 +147,17 @@
     pairs = kv_heads // PAIR
     lanes = page_count * TILE
     tokens = tiles * lanes
-    for p in range(pairs):
-        for copy in token_copies(value_hbm, values_ref, value_sems, p, span):
-            copy.start()
+    half_tiles = tiles // 2
+    half = half_tiles * lanes
+    for p in range(0, pairs, 2):
+        for part in range(2):
+            for q in range(p, min(p + 2, pairs)):
+                for tile in range(part * half_tiles, (part + 1) * half_tiles):
+                    pltpu.make_async_copy(
+                        value_hbm.at[:, tile, :, pl.ds(q * span, span)],
+                        values_ref.at[q, tile], value_sems.at[2 * q + part],
+                    ).start()
+    pl.delay(1)
     me = me_ref[0]
     target = me * page_count + lax.broadcasted_iota(jnp.int32, (kv_heads, lanes), 1) // TILE
     picked = target < 0
@@ -189,17 +195,21 @@
             for later in range(k + 1, 3 if k < 3 else 5):
                 rest[later] = rest[later] - part
 
-    def product(p):
-        values = values_ref[p].reshape(tokens, span)
-        new_values = padded_rows(new_values_ref[:, p * span : (p + 1) * span])
-        weights = scaled_ref[p * PAIR : (p + 1) * PAIR].reshape(PAIR * rows, tokens + LANES)
-        half = tokens // 2
+    def product(p, part):
+        place = slice(part * half, (part + 1) * half)
+        values = values_ref[p, part * half_tiles : (part + 1) * half_tiles].reshape(half, span)
         weighted = jnp.dot(
-            weights[:, :half], values[:half], preferred_element_type=jnp.float32
-        ) + jnp.dot(
-            weights[:, half:], jnp.concatenate([values[half:], new_values], axis=0),
+            scaled_ref[p * PAIR : (p + 1) * PAIR, :, place].reshape(PAIR * rows, half), values,
             preferred_element_type=jnp.float32,
         )
+        if part == 0:
+            new_values = padded_rows(new_values_ref[:, p * span : (p + 1) * span])
+            sums_ref[p] = weighted + jnp.dot(
+                scaled_ref[p * PAIR : (p + 1) * PAIR, :, tokens:].reshape(PAIR * rows, LANES),
+                new_values, preferred_element_type=jnp.float32,
+            )
+            return
+        weighted = weighted + sums_ref[p]
         for k in range(PAIR):
             for i in range(pieces):
                 first_row = k * rows + i * share
@@ -211,12 +221,14 @@
         scale_head(h)
     for p in range(0, pairs, 2):
         both = range(p, min(p + 2, pairs))
-        for q in both:
-            wait_all(values_ref, value_sems, q)
-        for q in both:
-            product(q)
-        for h in range((p + 2) * PAIR, min((p + 4) * PAIR, kv_heads)):
-            scale_head(h)
+        later = list(range((p + 2) * PAIR, min((p + 4) * PAIR, kv_heads)))
+        for part in range(2):
+            for q in both:
+                wait_part(values_ref, value_sems, q, part)
+            for q in both:
+                product(q, part)
+            for h in later[part::2]:
+                scale_head(h)
     turned = padded_rows(stats[0]).T
     for i in range(pieces):
         part = turned if i == 0 else pltpu.roll(turned, LANES - i * share, 1)
@@ -310,7 +322,8 @@
             pltpu.VMEM((pairs, tiles, page_count, TILE, span), bf16),
             pltpu.VMEM((kv_heads, rows, tokens + LANES), bf16),
             pltpu.VMEM((kv_heads, lanes + LANES), f32),
-            dma((pairs,)),
+            pltpu.VMEM((pairs, PAIR * rows, span), f32),
+            dma((2 * pairs,)),
         ],
         compiler_params=limit,
         name="attend",

time: 42.2 us -> 41.1 us (0.974)
  Pallas kernels: 7.73 us -> 6.52 us
  waiting for transfers between devices: 2.66 us -> 3.33 us
  blocking collectives: 22.1 us -> 21.5 us
    pallas_call x1, Pallas kernels: 4.22 us -> 3.55 us  [on_device(): pl.pallas_call(lambda *refs: score_kernel(groups, *refs), out_shape=(pltp...]
    all_to_all x1, waiting for transfers between devices: 2.66 us -> 3.33 us  [exchange(): lax.all_to_all(pieces, 'page', split_axis=0, concat_axis=0, tiled=True)]
    all_to_all x2, blocking collectives: 22.1 us -> 21.5 us  [exchange(): lax.all_to_all(pieces, 'page', split_axis=0, concat_axis=0, tiled=True)]
    pallas_call x1, Pallas kernels: 3.2 us -> 2.66 us  [on_device(): pl.pallas_call(lambda *refs: attend_kernel(listed, *refs), out_shape=jax....]
  transfers between devices with their start and end apart: 1 -> 1, of which waited for: 1 -> 1; matrix products, arithmetic and copies ran while one was open for 0% -> 0% of each run, Pallas kernels for 10% -> 9%
where the time goes in v5:
time: 41.1 us; the launch traced here: 40.8 us
  blocking collectives  21.5 us (52%)
  starting transfers between devices  7.39 us (18%)
  Pallas kernels  6.52 us (16%)
  waiting for transfers between devices  3.33 us (8%)
  local copies, waits for them, and re-layouts  1.98 us (5%)
    all_to_all x2, blocking collectives, exchange(): lax.all_to_all(pieces, 'page', split_axis=0, concat_axis=0, tiled=True)  21.5 us
    all_to_all x1, starting transfers between devices, exchange(): lax.all_to_all(pieces, 'page', split_axis=0, concat_axis=0, tiled=True)  7.39 us
    pallas_call x1, Pallas kernels, on_device(): pl.pallas_call(lambda *refs: score_kernel(groups, *refs), out_shape=(pltp...  3.55 us
    all_to_all x1, waiting for transfers between devices, exchange(): lax.all_to_all(pieces, 'page', split_axis=0, concat_axis=0, tiled=True)  3.33 us
    pallas_call x1, Pallas kernels, on_device(): pl.pallas_call(lambda *refs: attend_kernel(listed, *refs), out_shape=jax....  2.66 us
  transfers between devices with their start and end apart: 1, of which 1 were waited for; matrix products, arithmetic and copies ran while one was open for 0% of the time, Pallas kernels for 9%

profile of v5, /device:TPU:0, one launch (start us, length us, event | category | flops | bytes accessed | tf_op | source)
XLA Modules:
  0.0 40.8 jit_solution(1309514620900236665)
XLA Ops:
  0.0 0.7 %pad.4 = s32[8,128]{1,0:T(8,128)S(1)} pad(s32[8,16]{1,0:T(8,128)} %param.11, s32[]{:T(128)} %constant.1.clone.1), padding=0_0x0_112 | pad | bytes 4612 | tf_op jit(solution)/shard_map/jit(_pad)/pad | solution.py:286
  0.7 0.6 %broadcast_in_dim.2 = s32[16,8,128]{2,1,0:T(8,128)} broadcast(s32[8,128]{1,0:T(8,128)S(1)} %pad.4), dimensions={1,2} | broadcast | bytes 69632 | tf_op jit(solution)/shard_map/broadcast_in_dim | solution.py:287
  1.3 7.4 %all-to-all-start = ((s32[16,8,128]{2,1,0:T(8,128)}), s32[16,8,128]{2,1,0:T(8,128)S(1)}, u32[]{:S(2)}, u32[]{:S(2)}) async-start(s32[16,8,128]{2,1,0:T(8,128)} %broadcast_in_dim.2), calls=%async_computation | async-start | bytes 131072 | tf_op jit(solution)/shard_map/all_to_all | solution.py:261
  8.7 3.5 %scores.1 = (bf16[8,64,2176]{2,1,0:T(8,128)(2,1)S(1)}, f32[8,64,384]{2,1,0:T(8,128)S(1)}, bf16[16,1024]{1,0:T(8,128)(2,1)S(1)}) custom-call(bf16[16,4096]{1,0:T(8,128)(2,1)} %refs_0_.1, bf16[16,1024]{1,0:T(8,128)(2,1)} %refs_1_.1, bf16[16,1024]{1,0:T(8,128)(2,1)} %refs_2_.1, bf16[32,8,8,1024]{3,2,1,0:T(8,128)(2,1)} %bitcast.8), custom_call_target="tpu_custom_call" | custom-call | flops 268435456 | bytes 4194304 | tf_op jit(solution)/shard_map/scores/pallas_call | solution.py:288
  12.3 3.3 %all-to-all-done.refs_1_ = s32[16,8,128]{2,1,0:T(8,128)S(1)} async-done(((s32[16,8,128]{2,1,0:T(8,128)}), s32[16,8,128]{2,1,0:T(8,128)S(1)}, u32[]{:S(2)}, u32[]{:S(2)}) %all-to-all-start) | async-done | bytes 65568 | tf_op jit(solution)/shard_map/all_to_all | solution.py:261
  15.6 2.7 %attend.1 = bf16[16,40,128]{2,1,0:T(8,128)(2,1)S(1)} custom-call(s32[1]{0:T(128)} %bitcast.refs_0_, s32[16,8,128]{2,1,0:T(8,128)S(1)} %all-to-all-done.refs_1_, bf16[8,64,2176]{2,1,0:T(8,128)(2,1)S(1)} %get-tuple-element.8.refs_2_, f32[8,64,384]{2,1,0:T(8,128)S(1)} %get-tuple-element.9.refs_3_, bf16[16,1024]{1,0:T(8,128)(2,1)S(1)} %get-tuple-element.10.refs_4_, ...), custom_call_target="tpu_custom_call" | custom-call | tf_op jit(solution)/shard_map/attend/pallas_call | solution.py:316
  18.3 11.0 %all_to_all.15.pieces_ref = bf16[16,40,128]{2,1,0:T(8,128)(2,1)S(1)} all-to-all(bf16[16,40,128]{2,1,0:T(8,128)(2,1)S(1)} %attend.1), channel_id=1, replica_groups=mesh['grp'=2,'page'=16] {'page'}, dimensions={0} | all-to-all | bytes 327680 | tf_op jit(solution)/shard_map/all_to_all | solution.py:261
  29.3 0.3 merge.1
  29.6 10.5 %all_to_all.16 = bf16[16,32,128]{2,1,0:T(8,128)(2,1)S(1)} all-to-all(bf16[16,32,128]{2,1,0:T(8,128)(2,1)S(1)} %merge.1), channel_id=1, replica_groups=mesh['grp'=2,'page'=16] {'page'}, dimensions={0} | all-to-all | bytes 262144 | tf_op jit(solution)/shard_map/all_to_all | solution.py:261
  40.1 0.7 %copy.8 = bf16[16,4096]{1,0:T(8,128)(2,1)} copy(bf16[16,4096]{1,0:T(8,128)(2,1)S(1)} %bitcast.10) | data formatting | bytes 262144
Async XLA Ops:
  1.3 14.3 %all-to-all-start = ((s32[16,8,128]{2,1,0:T(8,128)}), s32[16,8,128]{2,1,0:T(8,128)S(1)}, u32[]{:S(2)}, u32[]{:S(2)}) async-start(s32[16,8,128]{2,1,0:T(8,128)} %broadcast_in_dim.2), calls=%async_computation | async-start | bytes 131072 | tf_op jit(solution)/shard_map/all_to_all | solution.py:261

commit v6 on v5

--- a/solution.py
+++ b/solution.py
@@ -23,6 +23,11 @@
 
 def keep_in(space, *arrays):
     return [pltpu.with_memory_space_constraint(array, space) for array in arrays]
+
+
+def destination(head, part, kv_heads, share, block):
+    tile, rest = divmod(part * share, block)
+    return (tile * kv_heads * block + head * block + rest) // share
 
 
 def padded_rows(rows):
@@ -134,7 +139,7 @@
 
 
 def attend_kernel(
-    listed, me_ref, chosen_ref, weights_ref, peaks_ref, new_values_ref, value_hbm,
+    listed, target, me_ref, chosen_ref, weights_ref, peaks_ref, new_values_ref, value_hbm,
     out_ref,
     values_ref, scaled_ref, bias_ref, sums_ref, value_sems,
 ):
@@ -159,13 +164,13 @@
                     ).start()
     pl.delay(1)
     me = me_ref[0]
-    target = me * page_count + lax.broadcasted_iota(jnp.int32, (kv_heads, lanes), 1) // TILE
-    picked = target < 0
+    page = me * page_count + lax.broadcasted_iota(jnp.int32, (kv_heads, lanes), 1) // TILE
+    picked = page < 0
     for d in range(devices):
         chosen = chosen_ref[d]
         for j in range(listed):
             column = jnp.broadcast_to(chosen[:, j : j + 1], (kv_heads, lanes))
-            picked = jnp.logical_or(picked, column == target)
+            picked = jnp.logical_or(picked, column == page)
     bias_ref[:, :lanes] = jnp.where(picked, 0.0, ABSENT)
     bias_ref[:, lanes:] = jnp.full((kv_heads, LANES), jnp.where(me == 0, 0.0, ABSENT))
     column = lax.broadcasted_iota(jnp.int32, (rows, LANES), 1)
@@ -213,7 +218,7 @@
         for k in range(PAIR):
             for i in range(pieces):
                 first_row = k * rows + i * share
-                out_ref[i * kv_heads + p * PAIR + k, :share, :] = weighted[
+                out_ref[target(p * PAIR + k, i), :share, :] = weighted[
                     first_row : first_row + share, k * width : (k + 1) * width
                 ].astype(jnp.bfloat16)
 
@@ -234,7 +239,7 @@
         part = turned if i == 0 else pltpu.roll(turned, LANES - i * share, 1)
         part = part.astype(jnp.bfloat16)
         for h in range(kv_heads):
-            out_ref[i * kv_heads + h, share:, :] = part[h * STATS : (h + 1) * STATS]
+            out_ref[target(h, i), share:, :] = part[h * STATS : (h + 1) * STATS]
 
 
 def merge_kernel(pieces_ref, out_ref):
@@ -281,6 +286,11 @@
     limit = pltpu.CompilerParams(vmem_limit_bytes=24 * 2**20)
     key_cache = key_cache.reshape(page_count, tiles, TILE, head_span)
     value_cache = value_cache.reshape(page_count, tiles, TILE, head_span)
+
+    block = groups * TILE
+
+    def target(head, part):
+        return destination(head, part, kv_heads, share, block)
 
     me = lax.axis_index("page").astype(jnp.int32).reshape(1)
     listing = jnp.pad(chosen, ((0, 0), (0, LANES - listed)), constant_values=-1)
@@ -314,7 +324,7 @@
     value_cache, = keep_in(pltpu.HBM, value_cache)
     resting = keep_in(pltpu.VMEM, chosen_all, weights, peaks, new_values)
     pieces = pl.pallas_call(
-        lambda *refs: attend_kernel(listed, *refs),
+        lambda *refs: attend_kernel(listed, target, *refs),
         out_shape=jax.ShapeDtypeStruct((devices, share + STATS, width), bf16),
         in_specs=[pl.BlockSpec(memory_space=pltpu.SMEM)] + [vmem()] * 4 + [hbm()],
         out_specs=vmem(),

time: 41.1 us -> 41.1 us (level)
  no operation moved by 1% of the time
where the time goes in v6:
time: 41.1 us; the launch traced here: 40.8 us
  blocking collectives  21.5 us (52%)
  starting transfers between devices  7.39 us (18%)
  Pallas kernels  6.52 us (16%)
  waiting for transfers between devices  3.33 us (8%)
  local copies, waits for them, and re-layouts  1.98 us (5%)
    all_to_all x2, blocking collectives, exchange(): lax.all_to_all(pieces, 'page', split_axis=0, concat_axis=0, tiled=True)  21.5 us
    all_to_all x1, starting transfers between devices, exchange(): lax.all_to_all(pieces, 'page', split_axis=0, concat_axis=0, tiled=True)  7.39 us
    pallas_call x1, Pallas kernels, on_device(): pl.pallas_call(lambda *refs: score_kernel(groups, *refs), out_shape=(pltp...  3.55 us
    all_to_all x1, waiting for transfers between devices, exchange(): lax.all_to_all(pieces, 'page', split_axis=0, concat_axis=0, tiled=True)  3.33 us
    pallas_call x1, Pallas kernels, on_device(): pl.pallas_call(lambda *refs: attend_kernel(listed, target, *refs), out_sh...  2.66 us
  transfers between devices with their start and end apart: 1, of which 1 were waited for; matrix products, arithmetic and copies ran while one was open for 0% of the time, Pallas kernels for 9%

profile of v6, /device:TPU:0, one launch (start us, length us, event | category | flops | bytes accessed | tf_op | source)
XLA Modules:
  0.0 40.8 jit_solution(1309514620900236665)
XLA Ops:
  0.0 0.7 %pad.4 = s32[8,128]{1,0:T(8,128)S(1)} pad(s32[8,16]{1,0:T(8,128)} %param.11, s32[]{:T(128)} %constant.1.clone.1), padding=0_0x0_112 | pad | bytes 4612 | tf_op jit(solution)/shard_map/jit(_pad)/pad | solution.py:296
  0.7 0.6 %broadcast_in_dim.2 = s32[16,8,128]{2,1,0:T(8,128)} broadcast(s32[8,128]{1,0:T(8,128)S(1)} %pad.4), dimensions={1,2} | broadcast | bytes 69632 | tf_op jit(solution)/shard_map/broadcast_in_dim | solution.py:297
  1.3 7.4 %all-to-all-start = ((s32[16,8,128]{2,1,0:T(8,128)}), s32[16,8,128]{2,1,0:T(8,128)S(1)}, u32[]{:S(2)}, u32[]{:S(2)}) async-start(s32[16,8,128]{2,1,0:T(8,128)} %broadcast_in_dim.2), calls=%async_computation | async-start | bytes 131072 | tf_op jit(solution)/shard_map/all_to_all | solution.py:266
  8.7 3.5 %scores.1 = (bf16[8,64,2176]{2,1,0:T(8,128)(2,1)S(1)}, f32[8,64,384]{2,1,0:T(8,128)S(1)}, bf16[16,1024]{1,0:T(8,128)(2,1)S(1)}) custom-call(bf16[16,4096]{1,0:T(8,128)(2,1)} %refs_0_.1, bf16[16,1024]{1,0:T(8,128)(2,1)} %refs_1_.1, bf16[16,1024]{1,0:T(8,128)(2,1)} %refs_2_.1, bf16[32,8,8,1024]{3,2,1,0:T(8,128)(2,1)} %bitcast.8), custom_call_target="tpu_custom_call" | custom-call | flops 268435456 | bytes 4194304 | tf_op jit(solution)/shard_map/scores/pallas_call | solution.py:298
  12.3 3.3 %all-to-all-done.refs_1_ = s32[16,8,128]{2,1,0:T(8,128)S(1)} async-done(((s32[16,8,128]{2,1,0:T(8,128)}), s32[16,8,128]{2,1,0:T(8,128)S(1)}, u32[]{:S(2)}, u32[]{:S(2)}) %all-to-all-start) | async-done | bytes 65568 | tf_op jit(solution)/shard_map/all_to_all | solution.py:266
  15.6 2.7 %attend.1 = bf16[16,40,128]{2,1,0:T(8,128)(2,1)S(1)} custom-call(s32[1]{0:T(128)} %bitcast.refs_0_, s32[16,8,128]{2,1,0:T(8,128)S(1)} %all-to-all-done.refs_1_, bf16[8,64,2176]{2,1,0:T(8,128)(2,1)S(1)} %get-tuple-element.8.refs_2_, f32[8,64,384]{2,1,0:T(8,128)S(1)} %get-tuple-element.9.refs_3_, bf16[16,1024]{1,0:T(8,128)(2,1)S(1)} %get-tuple-element.10.refs_4_, ...), custom_call_target="tpu_custom_call" | custom-call | tf_op jit(solution)/shard_map/attend/pallas_call | solution.py:326
  18.3 11.0 %all_to_all.15.pieces_ref = bf16[16,40,128]{2,1,0:T(8,128)(2,1)S(1)} all-to-all(bf16[16,40,128]{2,1,0:T(8,128)(2,1)S(1)} %attend.1), channel_id=1, replica_groups=mesh['grp'=2,'page'=16] {'page'}, dimensions={0} | all-to-all | bytes 327680 | tf_op jit(solution)/shard_map/all_to_all | solution.py:266
  29.3 0.3 merge.1
  29.6 10.5 %all_to_all.16 = bf16[16,32,128]{2,1,0:T(8,128)(2,1)S(1)} all-to-all(bf16[16,32,128]{2,1,0:T(8,128)(2,1)S(1)} %merge.1), channel_id=1, replica_groups=mesh['grp'=2,'page'=16] {'page'}, dimensions={0} | all-to-all | bytes 262144 | tf_op jit(solution)/shard_map/all_to_all | solution.py:266
  40.1 0.7 %copy.8 = bf16[16,4096]{1,0:T(8,128)(2,1)} copy(bf16[16,4096]{1,0:T(8,128)(2,1)S(1)} %bitcast.10) | data formatting | bytes 262144
Async XLA Ops:
  1.3 14.3 %all-to-all-start = ((s32[16,8,128]{2,1,0:T(8,128)}), s32[16,8,128]{2,1,0:T(8,128)S(1)}, u32[]{:S(2)}, u32[]{:S(2)}) async-start(s32[16,8,128]{2,1,0:T(8,128)} %broadcast_in_dim.2), calls=%async_computation | async-start | bytes 131072 | tf_op jit(solution)/shard_map/all_to_all | solution.py:266
